TPU v7x, 256 devices: a 4x2x16 block of a 4x16x16 slice. The times are simulated.
256 devices in a mesh: win: 2 (over y), row: 128 (over x, z, core).
Axes of the slice: x: 4, y: 2, z: 16, core: 2. Of those that a mesh axis runs over, the one named last changes fastest.
The devices are a block of a 4x16x16 slice.
Arguments:
- spectra: bfloat16 [256, 2, 32768], P(('win', 'row')), parts along dimension 0, may hold values from -6 to 6
- pair_mask: int32 [128, 128], P('row'), may hold values from 0 to 1, as said below
- available: int32 [256], P('win'), parts along dimension 0, may hold values 0 or 1
Outputs:
- correlations: float32 [256, 128, 8192], P(('win', 'row')), parts along dimension 0
There are 2 independent parts, one for each index of `win`. A program takes and returns all parts, laid end to end along the dimension named above; an argument that names none is the same for every part. Nothing has to cross between parts.
Inputs may be any that keep to these rules, and one draw needn't show every extreme that they name: pair_mask[i, j] is 0 wherever j <= i.
All inputs are finite; a program needn't handle non-finite values.
Results may differ from a plain program's by a relative error of at most 0.0003.
Values may be sent and summed in bfloat16 or wider, within the bound.
No kernel may reach another device: no remote copies, remote signals or barrier semaphores. Data moves between devices by JAX's collectives and lax.ppermute only.
A program may use at most 128 MiB of HBM per device.

v0:
```python
import functools
import math

import jax
import jax.numpy as jnp
import numpy as np
from jax import lax
from jax.experimental import pallas as pl
from jax.experimental.pallas import tpu as pltpu
from jax.sharding import PartitionSpec as P


LAGS = 8192
CORES = 2
ACROSS = 4
INNER = 128
CHAINS = 1


def split_table(table):
    high = table.astype(jnp.bfloat16)
    low = (table - high.astype(np.float64)).astype(jnp.bfloat16)
    return high, low


@functools.cache
def build_tables(freq):
    nfft = 2 * freq
    column = nfft // INNER
    depth = freq // column
    width = column // 2
    outer = LAGS // INNER
    scale = 2.0 / math.sqrt(8.0 * freq)
    lag = np.arange(INNER)[:, None]
    angle = 2.0 * np.pi * ((lag * np.arange(depth)[None, :]) % INNER) / INNER
    after = 2.0 * np.pi * ((lag * (np.arange(depth)[None, :] + 1)) % INNER) / INNER
    section = np.block(
        [
            [np.cos(angle), -np.sin(angle), np.cos(after), -np.sin(after)],
            [np.sin(angle), np.cos(angle), -np.sin(after), -np.cos(after)],
        ]
    )
    first = np.concatenate(split_table(section), axis=0)
    twist = 2.0 * np.pi * ((lag * np.arange(width)[None, :]) % nfft) / nfft
    turn = np.stack([np.cos(twist), np.sin(twist)]).astype(np.float32)
    steps = np.arange(outer)[None, :] - outer // 2
    angle = 2.0 * np.pi * ((np.arange(width)[:, None] * steps) % column) / column
    section = np.concatenate([np.cos(angle), -np.sin(angle)], axis=0) * scale
    second = np.concatenate(split_table(section), axis=1)
    odd = 2 * np.arange(depth)[:, None] + 1
    angle = 2.0 * np.pi * ((odd * lag.T) % (2 * INNER)) / (2 * INNER)
    section = np.concatenate([np.cos(angle), -np.sin(angle)], axis=0) * scale
    middle = np.concatenate(split_table(section), axis=1)
    wide = np.concatenate([second[:width], second[width:]], axis=1)
    return np.concatenate([first, wide, middle], axis=0), turn


def fold_body(whole_ref, *refs):
    many = (len(refs) - 2) // 2
    sources, out_ref, copied, sems = refs[:many], refs[many], refs[many + 1 : -1], refs[-1]
    copies = [
        pltpu.make_async_copy(source, target, sems.at[n])
        for n, (source, target) in enumerate(zip(sources, copied))
    ]
    for copy in copies:
        copy.start()
    rows, column = whole_ref.shape
    width = column // 2
    half = rows // 2
    whole = whole_ref[...]
    right = whole[:, width:]
    down = lax.broadcasted_iota(jnp.int32, (width, width), 0)
    over = lax.broadcasted_iota(jnp.int32, (width, width), 1)
    mirror = jnp.where(down == lax.rem(width - over, width), 1.0, 0.0).astype(jnp.bfloat16)
    flipped = jnp.dot(right, mirror, preferred_element_type=jnp.float32).astype(jnp.bfloat16)
    out_ref[pl.ds(0, rows), :] = whole[:, :width]
    out_ref[pl.ds(rows, rows), :] = flipped
    extra = out_ref.shape[0] - 2 * rows
    over = lax.broadcasted_iota(jnp.int32, (extra, width), 1)
    pick = jnp.where(over == 0, 1.0, 0.0).astype(jnp.bfloat16)
    straight = lax.dot_general(
        pick, right, (((1,), (1,)), ((), ())), preferred_element_type=jnp.float32
    )
    crossed = jnp.concatenate([straight[:, half:], -straight[:, :half]], axis=1)
    out_ref[pl.ds(2 * rows, extra), :] = jnp.concatenate([straight, crossed], axis=1).astype(
        jnp.bfloat16
    )
    for copy in copies:
        copy.wait()


def fold_call(whole, tables):
    rows, column = whole.shape
    vmem = pl.BlockSpec(memory_space=pltpu.VMEM)
    hbm = pl.BlockSpec(memory_space=pltpu.HBM)
    own = jax.ShapeDtypeStruct((2 * rows + 16, column // 2), jnp.bfloat16)
    return pl.pallas_call(
        fold_body,
        out_shape=[own] + [jax.ShapeDtypeStruct(table.shape, table.dtype) for table in tables],
        in_specs=[vmem] + [hbm] * len(tables),
        out_specs=[vmem] * (1 + len(tables)),
        scratch_shapes=[pltpu.SemaphoreType.DMA((len(tables),))],
        cost_estimate=pl.CostEstimate(flops=1_000_000, bytes_accessed=300_000, transcendentals=0),
        compiler_params=pltpu.CompilerParams(vmem_limit_bytes=16 * 1024 * 1024),
        name="fold",
    )(whole, *tables)


def split(value):
    high = value.astype(jnp.bfloat16)
    return high, (value - high.astype(jnp.float32)).astype(jnp.bfloat16)


def cross_spectrum(other, mine):
    parts = []
    quarter = mine.shape[0] // 4
    for n in (0, 2):
        ar, ai = mine[n * quarter : (n + 1) * quarter], mine[(n + 1) * quarter : (n + 2) * quarter]
        br, bi = other[n * quarter : (n + 1) * quarter], other[(n + 1) * quarter : (n + 2) * quarter]
        parts += [ar * br + ai * bi, ar * bi - ai * br]
    return jnp.concatenate(parts, axis=0)


def turned_columns(high, low, table, turn):
    wide = jnp.dot(table[: 4 * INNER], high, preferred_element_type=jnp.float32)
    rest = jnp.dot(table[: 2 * INNER], low, preferred_element_type=jnp.float32)
    mixed = wide[: 2 * INNER] + wide[2 * INNER :] + rest
    sr, si = mixed[:INNER], mixed[INNER:]
    tc, ts = turn[0], turn[1]
    turned = jnp.concatenate([sr * tc - si * ts, sr * ts + si * tc], axis=1)
    return split(turned)


def lags_of(summed, middle):
    summed = summed.T
    outer = summed.shape[0] // 2
    parity = lax.broadcasted_iota(jnp.int32, (outer, INNER), 0) % 2
    return summed[:outer] + summed[outer:] + jnp.where(parity == 0, middle, -middle)


def stage_body(step, plan, along, pair_at, info, own_w, pair_w, mine0, mine1, table, turn, *rest):
    chains = CHAINS
    slab_count = chains * sum(present for present, _ in plan)
    slabs, rest = rest[:slab_count], rest[-11:]
    own_hbm, pair_hbm, token, held, wide, mids, kept, result_ref, listed, names, sems = rest
    token[...] = jnp.zeros_like(token)
    x, z, c = info[0], info[1], info[2]
    sign = 2 * c - 1
    part = slabs[0].shape[0]
    per = chains * part
    size = wide.shape[1]
    count = jnp.int32(0)
    taken = 0
    for side, (present, rows) in enumerate(plan):
        if not present:
            continue
        for chain in range(chains):
            held[pl.ds(side * per + chain * part, part)] = slabs[taken][...]
            taken += 1
        zj = lax.rem(z + sign * (step - side) + along, along)
        for n in range(per):
            e = side * per + n
            xj = lax.rem(x + side * sign + 2 * (n % 2) + ACROSS, ACROSS)
            j = (xj * along + zj) * CORES + lax.rem(c + n // 2, CORES)
            names[e] = j
            for row in range(rows):
                listed[count] = e * 2 + row
                keep = (own_w if row == 0 else pair_w)[j] != 0.0
                count = count + keep.astype(jnp.int32)

    quarter = size // 4
    down = lax.broadcasted_iota(jnp.int32, wide.shape[1:], 0)
    over = lax.broadcasted_iota(jnp.int32, wide.shape[1:], 1)
    once = (over == 0) & ((down == 0) | (down == quarter))
    weight = jnp.where(once, 0.5, jnp.where((over == 0) & (down >= 2 * quarter), 0.0, 1.0))
    lane = lax.broadcasted_iota(jnp.int32, (2 * per, INNER), 1)
    spot = lax.broadcasted_iota(jnp.int32, (2 * per, INNER), 0)
    straight = jnp.zeros((2 * per, INNER), jnp.float32)
    crossed = jnp.zeros((2 * per, INNER), jnp.float32)
    for side, (present, rows) in enumerate(plan):
        for e in range(side * per, (side + 1) * per if present else 0):
            edge = held[e, size:].astype(jnp.float32)[: 2 * per]
            straight = jnp.where(spot == e, edge[:, :INNER], straight)
            crossed = jnp.where(spot == e, edge[:, INNER:], crossed)
    parts = []
    for row in range(2):
        mine = mine1 if row else mine0
        wide[row] = mine[:size].astype(jnp.float32) * weight
        edge = mine[size:].astype(jnp.float32)[: 2 * per]
        real = jnp.where(lane < INNER // 2, edge[:, :INNER], -edge[:, INNER:])
        imag = jnp.where(lane < INNER // 2, edge[:, INNER:], edge[:, :INNER])
        parts.append(real * straight + imag * crossed)
    high, low = split(jnp.concatenate(parts, axis=0))
    rows_of = high.shape[0]
    summed = jnp.dot(
        jnp.concatenate([high, low], axis=0), table[6 * INNER :], preferred_element_type=jnp.float32
    )
    summed = summed[:rows_of] + summed[rows_of:]
    mids[...] = summed[:, :INNER] + summed[:, INNER:]

    def copy_out(code):
        e = code // 2
        return pltpu.make_async_copy(result_ref.at[code], own_hbm.at[names[e]], sems.at[code])

    def copy_pair(code):
        to = pair_hbm.at[pair_at + code // 2]
        return pltpu.make_async_copy(result_ref.at[code], to, sems.at[code])

    def columns(code):
        other = held[code // 2, :size].astype(jnp.float32)
        return turned_columns(*split(cross_spectrum(other, wide[code % 2])), table, turn)

    def middle_of(code):
        return mids[pl.ds(lax.rem(code, 2) * 2 * per + code // 2, 1), :]

    def keep_result(code, value):
        result_ref[code] = value

        @pl.when(code % 2 == 0)
        def _():
            copy_out(code).start()

        if pair_hbm is not None:
            @pl.when(code % 2 != 0)
            def _():
                copy_pair(code).start()

    def codes(k):
        return listed[2 * k], listed[jnp.minimum(2 * k + 1, count - 1)]

    def turn_two(k):
        code0, code1 = codes(k)
        kept[...] = jnp.concatenate([*columns(code0), *columns(code1)], axis=0)

    def sum_two(k):
        code0, code1 = codes(k)
        cosine = table[4 * INNER : 6 * INNER, :INNER]
        sine = table[4 * INNER : 6 * INNER, INNER:]
        summed = jnp.dot(kept[:, : 2 * INNER], cosine, preferred_element_type=jnp.float32)
        summed += jnp.dot(kept[:, 2 * INNER :], sine, preferred_element_type=jnp.float32)
        value0 = lags_of(summed[:INNER] + summed[INNER : 2 * INNER], middle_of(code0))
        value1 = lags_of(summed[2 * INNER : 3 * INNER] + summed[3 * INNER :], middle_of(code1))
        return value0, value1

    def keep_two(k, value0, value1):
        code0, code1 = codes(k)
        keep_result(code0, value0)

        @pl.when(2 * k + 1 < count)
        def _():
            keep_result(code1, value1)

    def both(k, _):
        last = jnp.maximum(k - 1, 0)
        values = sum_two(last)
        turn_two(jnp.minimum(k, twos - 1))

        @pl.when(k > 0)
        def _():
            keep_two(last, *values)

        return 0

    twos = (count + 1) // 2
    lax.fori_loop(0, jnp.where(count > 0, twos + 1, 0), both, 0)
    for side, (present, rows) in enumerate(plan):
        for e in range(side * per, (side + 1) * per if present else 0):
            @pl.when(own_w[names[e]] != 0.0)
            def _():
                copy_out(2 * e).wait()

            if rows > 1:
                @pl.when(pair_w[names[e]] != 0.0)
                def _():
                    copy_pair(2 * e + 1).wait()


def stage_call(step, plan, along, slabs, info, own_w, pair_w, mine, tables, own_buf, pair_buf, pair_at, pair_size):
    total = own_w.shape[0]
    count = 2 * CHAINS * slabs[0].shape[0]
    outer = LAGS // INNER
    smem = pl.BlockSpec(memory_space=pltpu.SMEM)
    vmem = pl.BlockSpec(memory_space=pltpu.VMEM)
    hbm = pl.BlockSpec(memory_space=pl.ANY)
    args = [info, own_w, pair_w, *mine, *tables, *slabs]
    specs = [smem] * 3 + [vmem] * (2 + len(tables) + len(slabs))
    used = len(args)
    out_shape = [jax.ShapeDtypeStruct((8, INNER), jnp.float32)]
    out_shape.append(jax.ShapeDtypeStruct((total, outer, INNER), jnp.float32))
    out_specs = [vmem, hbm]
    aliases = {}
    if own_buf is not None:
        aliases[len(args)] = 1
        args.append(own_buf)
        specs.append(hbm)
    with_pair = pair_size is not None
    if with_pair:
        out_shape.append(jax.ShapeDtypeStruct((pair_size, outer, INNER), jnp.float32))
        out_specs.append(hbm)
        if pair_buf is not None:
            aliases[len(args)] = 2
            args.append(pair_buf)
            specs.append(hbm)

    def body(*refs):
        scratch = refs[-8:]
        outs = refs[len(args) : -8]
        pair_ref = outs[2] if with_pair else None
        stage_body(step, plan, along, pair_at, *refs[:used], outs[1], pair_ref, outs[0], *scratch)

    flops = sum(rows * count // 2 for present, rows in plan if present) * 100_000_000
    return pl.pallas_call(
        body,
        out_shape=out_shape,
        in_specs=specs,
        out_specs=out_specs,
        scratch_shapes=[
            pltpu.VMEM((count,) + mine[0].shape, jnp.bfloat16),
            pltpu.VMEM((2, 2 * INNER, mine[0].shape[1]), jnp.float32),
            pltpu.VMEM((2 * count, INNER), jnp.float32),
            pltpu.VMEM((4 * INNER, 2 * mine[0].shape[1]), jnp.bfloat16),
            pltpu.VMEM((2 * count, outer, INNER), jnp.float32),
            pltpu.SMEM((2 * count + 1,), jnp.int32),
            pltpu.SMEM((count,), jnp.int32),
            pltpu.SemaphoreType.DMA((2 * count,)),
        ],
        input_output_aliases=aliases,
        cost_estimate=pl.CostEstimate(flops=flops, bytes_accessed=3_000_000, transcendentals=0),
        compiler_params=pltpu.CompilerParams(vmem_limit_bytes=16 * 1024 * 1024),
    )(*args)


def finish_body(src_ref, own_w, own_ref, early_ref, late_ref, out_ref, lines):
    g = pl.program_id(0)
    first = early_ref.shape[0]
    block, outer = own_ref.shape[:2]
    pitch = outer + 8

    def tile(m, _):
        for k in range(8):
            j = g * block + m * 8 + k
            src = src_ref[j]
            live = own_w[j] != 0.0
            early = early_ref[jnp.clip(src, 0, first - 1)]
            late = late_ref[jnp.clip(src - first, 0, late_ref.shape[0] - 1)]
            value = jnp.where(src < 0, own_ref[m * 8 + k], jnp.where(src < first, early, late))
            lines[pl.ds(k * pitch, outer), :] = jnp.where(live, value, 0.0)
        for n in range(outer):
            to = pl.ds(pl.multiple_of(m * 8 * outer + 8 * n, 8), 8)
            out_ref[to, :] = lines[pl.ds(n, 8, stride=pitch), :]
        return 0

    lax.fori_loop(0, block // 8, tile, 0)


def finish_call(src, own_w, own_buf, early, late):
    outer = LAGS // INNER
    total = src.shape[0]
    block = 32
    smem = pl.BlockSpec(memory_space=pltpu.SMEM)
    vmem = pl.BlockSpec(memory_space=pltpu.VMEM)
    return pl.pallas_call(
        finish_body,
        grid=(total // block,),
        out_shape=jax.ShapeDtypeStruct((total * outer, INNER), jnp.float32),
        in_specs=[smem, smem, pl.BlockSpec((block, outer, INNER), lambda g: (g, 0, 0)), vmem, vmem],
        out_specs=pl.BlockSpec((block * outer, INNER), lambda g: (g, 0)),
        scratch_shapes=[pltpu.VMEM((8 * (outer + 8), INNER), jnp.float32)],
        cost_estimate=pl.CostEstimate(flops=1_000_000, bytes_accessed=8_000_000, transcendentals=0),
        compiler_params=pltpu.CompilerParams(vmem_limit_bytes=16 * 1024 * 1024),
        name="finish",
    )(src, own_w, own_buf, early, late)


def per_device(total, spectra, pair_mask, available):
    along = total // (ACROSS * CORES)
    far = along // 2
    freq = spectra.shape[2]
    column = 2 * freq // INNER
    tables = [jnp.asarray(table) for table in build_tables(freq)]

    def move(value, goal_of):
        pairs = []
        for start in range(total):
            x, z, c = start // (along * CORES), start // CORES % along, start % CORES
            x, z, c = goal_of(x, z, c)
            pairs.append((start, (x % ACROSS * along + z % along) * CORES + c % CORES))
        return lax.ppermute(value, "row", pairs)

    def swap(value):
        return move(value, lambda x, z, c: (x, z, c + 1))

    def onward(value):
        return move(value, lambda x, z, c: (x, z + 1 - 2 * c, c))

    def sideways(value):
        return move(value, lambda x, z, c: (x + 1 - 2 * c, z, c))

    me = lax.axis_index("row")
    x, z, c = me // (along * CORES), me // CORES % along, me % CORES
    info = jnp.stack([x, z, c]).astype(jnp.int32)

    own, *tables = fold_call(spectra.reshape(2 * freq // column, column), tables)
    across = move(own, lambda x, z, c: (x + 2 - 4 * c, z, c))
    flag = lax.dynamic_slice_in_dim(available, me, 1, 0).astype(jnp.float32)
    own_w = pair_mask[0].astype(jnp.float32) * flag * available.astype(jnp.float32)
    pair_w = swap(own_w)
    other = swap(own)
    across, pair_w, other, info = lax.optimization_barrier((across, pair_w, other, info))
    pieces = [own, across, other, swap(across)]
    width = len(pieces) // CHAINS
    slab = tuple(jnp.stack(pieces[n * width : (n + 1) * width]) for n in range(CHAINS))
    mine = (own, other)

    cut = far - 2
    early = late = own_buf = side = None
    for step in range(far + 2):
        plan, slabs = [], []
        for value, stage in ((slab, step), (side, step - 1)):
            plan.append((value is not None, 2 if 0 < stage < far else 1))
            slabs += value or ()
        next_slab, beside = [], []
        for part in slab or ():
            if step < far:
                next_slab.append(onward(part))
        for part in slab or ():
            beside.append(sideways(part))
        side = tuple(beside) or None
        next_slab = tuple(next_slab) or None
        paired = 1 <= step <= far
        if paired and step <= cut:
            buf, at, size = early, 8 * (step - 1), 8 * cut
        elif paired:
            buf, at, size = late, 8 * (step - 1 - cut), 8 * (far - cut)
        else:
            buf, at, size = None, None, None
        token, own_buf, *pair_buf = stage_call(
            step, plan, along, slabs, info, own_w, pair_w, mine, tables, own_buf, buf, at, size
        )
        if paired and step <= cut:
            early = pair_buf[0]
        elif paired:
            late = pair_buf[0]

        def after(parts):
            return parts and tuple(lax.optimization_barrier((part, token))[0] for part in parts)

        slab, side = after(next_slab), side if step > far else after(side)
    early, late = swap(early), swap(late)

    j = lax.iota(jnp.int32, total)
    xj, zj, cj = j // (along * CORES), j // CORES % along, j % CORES
    dx, dz = (xj - x) % ACROSS, (zj - z) % along
    host = (dz < far).astype(jnp.int32)
    stage = jnp.where(dz < far, dz, along - dz)
    beside = dx % 2
    half = jnp.where(beside == 1, (dx + 1 - 2 * host) % ACROSS // 2, dx // 2)
    entry = 4 * beside + 2 * ((cj - host) % CORES) + half
    far_one = (host != c) & (dz != 0) & (dz != far)
    src = jnp.where(far_one, 8 * (stage - 1 + beside) + entry, -1).astype(jnp.int32)
    out = finish_call(src, own_w, own_buf, early, late)
    out = out.reshape(total // 8, LAGS // INNER, 8, INNER)
    return jnp.transpose(out, (0, 2, 1, 3)).reshape(1, total, LAGS)


def solution(mesh):
    total = mesh.shape["row"]

    def program(*args):
        return per_device(total, *args)

    return jax.shard_map(
        program,
        mesh=mesh,
        in_specs=(P(("win", "row"), None, None), P("row", None), P("win")),
        out_specs=P(("win", "row"), None, None),
        check_vma=False,
    )
```

profile of v0, /device:TPU:40, one launch (start us, length us, event | category | flops | bytes accessed | tf_op | source)
XLA Modules:
  0.0 137.0 jit_solution(9902278259176671337)
XLA Ops:
  0.0 1.0 reshape.12.whole_ref
  1.0 1.0 copy-done
  2.0 0.9 copy-done.1
  3.0 0.5 fold.1
  3.5 0.1 collective-permute-start.2
  3.6 3.4 %collective-permute-start = (bf16[272,256]{1,0:T(8,128)(2,1)S(1)}, bf16[272,256]{1,0:T(8,128)(2,1)S(1)}, u32[]{:S(2)}, u32[]{:S(2)}) collective-permute-start(bf16[272,256]{1,0:T(8,128)(2,1)S(1)} %get-tuple-element.54.refs_3_), channel_id=1, source_target_pairs={{0,64},{1,65},{2,66},{3,67},{4,68},{5,69},{6,70},{7,71},{8,72},{9,... | collective-permute-start | bytes 417800 | tf_op jit(solution)/shard_map/ppermute | solution.py:388
  7.1 1.2 dynamic_slice.3
  8.9 0.7 bitcast_multiply_fusion.refs_1_.own_w
  9.6 0.1 collective-permute-start.1
  9.7 0.1 pad_add_fusion.refs_0_
  9.8 1.0 collective-permute-done.1.refs_2_
  10.8 0.5 collective-permute-done
  11.3 1.4 collective-permute-done.3
  12.6 0.1 pad_maximum_fusion.refs_7_
  12.7 2.9 %collective-permute-start.4 = (bf16[4,272,256]{2,1,0:T(8,128)(2,1)S(1)}, bf16[4,272,256]{2,1,0:T(8,128)(2,1)S(1)}, u32[]{:S(2)}, u32[]{:S(2)}) collective-permute-start(bf16[4,272,256]{2,1,0:T(8,128)(2,1)S(1)} %pad_maximum_fusion.refs_7_), channel_id=1, source_target_pairs={{0,2},{1,31},{2,4},{3,1},{4,6},{5,3},{6,8},{7,5},{8,10},{9,7},{10,... | collective-permute-start | bytes 1671176 | tf_op jit(solution)/shard_map/ppermute | solution.py:388
  15.6 1.6 %collective-permute-start.6 = (bf16[4,272,256]{2,1,0:T(8,128)(2,1)S(1)}, bf16[4,272,256]{2,1,0:T(8,128)(2,1)S(1)}, u32[]{:S(2)}, u32[]{:S(2)}) collective-permute-start(bf16[4,272,256]{2,1,0:T(8,128)(2,1)S(1)} %pad_maximum_fusion.refs_7_), channel_id=1, source_target_pairs={{0,32},{1,97},{2,34},{3,99},{4,36},{5,101},{6,38},{7,103},{8,40},{... | collective-permute-start | bytes 1671176 | tf_op jit(solution)/shard_map/ppermute | solution.py:388
  17.2 3.5 %shard_map.55 = (f32[8,128]{1,0:T(8,128)}, f32[128,64,128]{2,1,0:T(8,128)S(1)}) custom-call(s32[3]{0:T(128)S(1)} %pad_add_fusion.refs_0_, f32[128]{0:T(128)S(1)} %bitcast_multiply_fusion.refs_1_.own_w, f32[128]{0:T(128)S(1)} %collective-permute-done.1.refs_2_, bf16[272,256]{1,0:T(8,128)(2,1)S(1)} %get-tuple-element.54.refs_3_, ...), custom_call_target="tpu_custom_call" | custom-call | flops 400000000 | bytes 3000000 | tf_op jit(solution)/shard_map/pallas_call | solution.py:312
  20.7 22.0 %collective-permute-done.4.refs_7_ = bf16[4,272,256]{2,1,0:T(8,128)(2,1)S(1)} collective-permute-done((bf16[4,272,256]{2,1,0:T(8,128)(2,1)S(1)}, bf16[4,272,256]{2,1,0:T(8,128)(2,1)S(1)}, u32[]{:S(2)}, u32[]{:S(2)}) %collective-permute-start.4) | collective-permute-done | bytes 557088 | tf_op jit(solution)/shard_map/ppermute | solution.py:388
  42.7 1.6 %collective-permute-start.8 = (bf16[4,272,256]{2,1,0:T(8,128)(2,1)S(1)}, bf16[4,272,256]{2,1,0:T(8,128)(2,1)S(1)}, u32[]{:S(2)}, u32[]{:S(2)}) collective-permute-start(bf16[4,272,256]{2,1,0:T(8,128)(2,1)S(1)} %collective-permute-done.4.refs_7_), channel_id=1, source_target_pairs={{0,32},{1,97},{2,34},{3,99},{4,36},{5,101},{6,38},{7,103},{8,40},{... | collective-permute-start | bytes 1671176 | tf_op jit(solution)/shard_map/ppermute | solution.py:388
  44.3 5.1 %shard_map.56 = (f32[8,128]{1,0:T(8,128)}, f32[128,64,128]{2,1,0:T(8,128)S(1)}, f32[48,64,128]{2,1,0:T(8,128)S(1)}) custom-call(s32[3]{0:T(128)S(1)} %pad_add_fusion.refs_0_, f32[128]{0:T(128)S(1)} %bitcast_multiply_fusion.refs_1_.own_w, f32[128]{0:T(128)S(1)} %collective-permute-done.1.refs_2_, ...), custom_call_target="tpu_custom_call", output_to_operand_aliasing={{1}: (9, {})} | custom-call | flops 1200000000 | bytes 3000000 | tf_op jit(solution)/shard_map/pallas_call | solution.py:312
  49.4 4.1 %collective-permute-done.5.refs_7_ = bf16[4,272,256]{2,1,0:T(8,128)(2,1)S(1)} collective-permute-done((bf16[4,272,256]{2,1,0:T(8,128)(2,1)S(1)}, bf16[4,272,256]{2,1,0:T(8,128)(2,1)S(1)}, u32[]{:S(2)}, u32[]{:S(2)}) %collective-permute-start.5) | collective-permute-done | bytes 557088 | tf_op jit(solution)/shard_map/ppermute | solution.py:388
  53.4 1.6 %collective-permute-start.10 = (bf16[4,272,256]{2,1,0:T(8,128)(2,1)S(1)}, bf16[4,272,256]{2,1,0:T(8,128)(2,1)S(1)}, u32[]{:S(2)}, u32[]{:S(2)}) collective-permute-start(bf16[4,272,256]{2,1,0:T(8,128)(2,1)S(1)} %collective-permute-done.5.refs_7_), channel_id=1, source_target_pairs={{0,32},{1,97},{2,34},{3,99},{4,36},{5,101},{6,38},{7,103},{8,40},{... | collective-permute-start | bytes 1671176 | tf_op jit(solution)/shard_map/ppermute | solution.py:388
  55.0 5.8 %shard_map.57 = (f32[8,128]{1,0:T(8,128)}, f32[128,64,128]{2,1,0:T(8,128)S(1)}, f32[48,64,128]{2,1,0:T(8,128)S(1)}) custom-call(s32[3]{0:T(128)S(1)} %pad_add_fusion.refs_0_, f32[128]{0:T(128)S(1)} %bitcast_multiply_fusion.refs_1_.own_w, f32[128]{0:T(128)S(1)} %collective-permute-done.1.refs_2_, ...), custom_call_target="tpu_custom_call", output_to_operand_aliasing={{1}: (9, {}), {2}: (10, {})} | custom-call | flops 1600000000 | bytes 3000000 | tf_op jit(solution)/shard_map/pallas_call | solution.py:312
  60.9 3.3 %collective-permute-done.7.refs_7_ = bf16[4,272,256]{2,1,0:T(8,128)(2,1)S(1)} collective-permute-done((bf16[4,272,256]{2,1,0:T(8,128)(2,1)S(1)}, bf16[4,272,256]{2,1,0:T(8,128)(2,1)S(1)}, u32[]{:S(2)}, u32[]{:S(2)}) %collective-permute-start.7) | collective-permute-done | bytes 557088 | tf_op jit(solution)/shard_map/ppermute | solution.py:388
  64.2 1.6 %collective-permute-start.12 = (bf16[4,272,256]{2,1,0:T(8,128)(2,1)S(1)}, bf16[4,272,256]{2,1,0:T(8,128)(2,1)S(1)}, u32[]{:S(2)}, u32[]{:S(2)}) collective-permute-start(bf16[4,272,256]{2,1,0:T(8,128)(2,1)S(1)} %collective-permute-done.7.refs_7_), channel_id=1, source_target_pairs={{0,32},{1,97},{2,34},{3,99},{4,36},{5,101},{6,38},{7,103},{8,40},{... | collective-permute-start | bytes 1671176 | tf_op jit(solution)/shard_map/ppermute | solution.py:388
  65.8 7.4 %shard_map.58 = (f32[8,128]{1,0:T(8,128)}, f32[128,64,128]{2,1,0:T(8,128)S(1)}, f32[48,64,128]{2,1,0:T(8,128)S(1)}) custom-call(s32[3]{0:T(128)S(1)} %pad_add_fusion.refs_0_, f32[128]{0:T(128)S(1)} %bitcast_multiply_fusion.refs_1_.own_w, f32[128]{0:T(128)S(1)} %collective-permute-done.1.refs_2_, ...), custom_call_target="tpu_custom_call", output_to_operand_aliasing={{1}: (9, {}), {2}: (10, {})} | custom-call | flops 1600000000 | bytes 3000000 | tf_op jit(solution)/shard_map/pallas_call | solution.py:312
  73.2 1.7 %collective-permute-done.9.refs_7_ = bf16[4,272,256]{2,1,0:T(8,128)(2,1)S(1)} collective-permute-done((bf16[4,272,256]{2,1,0:T(8,128)(2,1)S(1)}, bf16[4,272,256]{2,1,0:T(8,128)(2,1)S(1)}, u32[]{:S(2)}, u32[]{:S(2)}) %collective-permute-start.9) | collective-permute-done | bytes 557088 | tf_op jit(solution)/shard_map/ppermute | solution.py:388
  74.9 1.6 %collective-permute-start.14 = (bf16[4,272,256]{2,1,0:T(8,128)(2,1)S(1)}, bf16[4,272,256]{2,1,0:T(8,128)(2,1)S(1)}, u32[]{:S(2)}, u32[]{:S(2)}) collective-permute-start(bf16[4,272,256]{2,1,0:T(8,128)(2,1)S(1)} %collective-permute-done.9.refs_7_), channel_id=1, source_target_pairs={{0,32},{1,97},{2,34},{3,99},{4,36},{5,101},{6,38},{7,103},{8,40},{... | collective-permute-start | bytes 1671176 | tf_op jit(solution)/shard_map/ppermute | solution.py:388
  76.5 6.6 %shard_map.59 = (f32[8,128]{1,0:T(8,128)}, f32[128,64,128]{2,1,0:T(8,128)S(1)}, f32[48,64,128]{2,1,0:T(8,128)S(1)}) custom-call(s32[3]{0:T(128)S(1)} %pad_add_fusion.refs_0_, f32[128]{0:T(128)S(1)} %bitcast_multiply_fusion.refs_1_.own_w, f32[128]{0:T(128)S(1)} %collective-permute-done.1.refs_2_, ...), custom_call_target="tpu_custom_call", output_to_operand_aliasing={{1}: (9, {}), {2}: (10, {})} | custom-call | flops 1600000000 | bytes 3000000 | tf_op jit(solution)/shard_map/pallas_call | solution.py:312
  83.1 2.6 %collective-permute-done.11.refs_7_ = bf16[4,272,256]{2,1,0:T(8,128)(2,1)S(1)} collective-permute-done((bf16[4,272,256]{2,1,0:T(8,128)(2,1)S(1)}, bf16[4,272,256]{2,1,0:T(8,128)(2,1)S(1)}, u32[]{:S(2)}, u32[]{:S(2)}) %collective-permute-start.11) | collective-permute-done | bytes 557088 | tf_op jit(solution)/shard_map/ppermute | solution.py:388
  85.7 1.6 %collective-permute-start.16 = (bf16[4,272,256]{2,1,0:T(8,128)(2,1)S(1)}, bf16[4,272,256]{2,1,0:T(8,128)(2,1)S(1)}, u32[]{:S(2)}, u32[]{:S(2)}) collective-permute-start(bf16[4,272,256]{2,1,0:T(8,128)(2,1)S(1)} %collective-permute-done.11.refs_7_), channel_id=1, source_target_pairs={{0,32},{1,97},{2,34},{3,99},{4,36},{5,101},{6,38},{7,103},{8,40},{... | collective-permute-start | bytes 1671176 | tf_op jit(solution)/shard_map/ppermute | solution.py:388
  87.3 6.6 %shard_map.60 = (f32[8,128]{1,0:T(8,128)}, f32[128,64,128]{2,1,0:T(8,128)S(1)}, f32[48,64,128]{2,1,0:T(8,128)S(1)}) custom-call(s32[3]{0:T(128)S(1)} %pad_add_fusion.refs_0_, f32[128]{0:T(128)S(1)} %bitcast_multiply_fusion.refs_1_.own_w, f32[128]{0:T(128)S(1)} %collective-permute-done.1.refs_2_, ...), custom_call_target="tpu_custom_call", output_to_operand_aliasing={{1}: (9, {}), {2}: (10, {})} | custom-call | flops 1600000000 | bytes 3000000 | tf_op jit(solution)/shard_map/pallas_call | solution.py:312
  93.9 2.5 %collective-permute-done.13.refs_7_ = bf16[4,272,256]{2,1,0:T(8,128)(2,1)S(1)} collective-permute-done((bf16[4,272,256]{2,1,0:T(8,128)(2,1)S(1)}, bf16[4,272,256]{2,1,0:T(8,128)(2,1)S(1)}, u32[]{:S(2)}, u32[]{:S(2)}) %collective-permute-start.13) | collective-permute-done | bytes 557088 | tf_op jit(solution)/shard_map/ppermute | solution.py:388
  96.4 4.4 %shard_map.61 = (f32[8,128]{1,0:T(8,128)}, f32[128,64,128]{2,1,0:T(8,128)S(1)}, f32[48,64,128]{2,1,0:T(8,128)S(1)}) custom-call(s32[3]{0:T(128)S(1)} %pad_add_fusion.refs_0_, f32[128]{0:T(128)S(1)} %bitcast_multiply_fusion.refs_1_.own_w, f32[128]{0:T(128)S(1)} %collective-permute-done.1.refs_2_, ...), custom_call_target="tpu_custom_call", output_to_operand_aliasing={{1}: (9, {}), {2}: (10, {})} | custom-call | flops 1600000000 | bytes 3000000 | tf_op jit(solution)/shard_map/pallas_call | solution.py:312
  100.9 0.1 collective-permute-start.21
  101.0 1.0 collective-permute-start.18
  102.0 5.2 %collective-permute-done.15.refs_7_ = bf16[4,272,256]{2,1,0:T(8,128)(2,1)S(1)} collective-permute-done((bf16[4,272,256]{2,1,0:T(8,128)(2,1)S(1)}, bf16[4,272,256]{2,1,0:T(8,128)(2,1)S(1)}, u32[]{:S(2)}, u32[]{:S(2)}) %collective-permute-start.15) | collective-permute-done | bytes 557088 | tf_op jit(solution)/shard_map/ppermute | solution.py:388
  107.2 1.6 %collective-permute-start.20 = (bf16[4,272,256]{2,1,0:T(8,128)(2,1)S(1)}, bf16[4,272,256]{2,1,0:T(8,128)(2,1)S(1)}, u32[]{:S(2)}, u32[]{:S(2)}) collective-permute-start(bf16[4,272,256]{2,1,0:T(8,128)(2,1)S(1)} %collective-permute-done.15.refs_7_), channel_id=1, source_target_pairs={{0,32},{1,97},{2,34},{3,99},{4,36},{5,101},{6,38},{7,103},{8,40},{... | collective-permute-start | bytes 1671176 | tf_op jit(solution)/shard_map/ppermute | solution.py:388
  108.7 3.1 %collective-permute-done.18.refs_8_ = bf16[4,272,256]{2,1,0:T(8,128)(2,1)S(1)} collective-permute-done((bf16[4,272,256]{2,1,0:T(8,128)(2,1)S(1)}, bf16[4,272,256]{2,1,0:T(8,128)(2,1)S(1)}, u32[]{:S(2)}, u32[]{:S(2)}) %collective-permute-start.18) | collective-permute-done | bytes 557088 | tf_op jit(solution)/shard_map/ppermute | solution.py:388
  111.9 4.4 %shard_map.62 = (f32[8,128]{1,0:T(8,128)}, f32[128,64,128]{2,1,0:T(8,128)S(1)}, f32[16,64,128]{2,1,0:T(8,128)S(1)}) custom-call(s32[3]{0:T(128)S(1)} %pad_add_fusion.refs_0_, f32[128]{0:T(128)S(1)} %bitcast_multiply_fusion.refs_1_.own_w, f32[128]{0:T(128)S(1)} %collective-permute-done.1.refs_2_, ...), custom_call_target="tpu_custom_call", output_to_operand_aliasing={{1}: (9, {})} | custom-call | flops 1600000000 | bytes 3000000 | tf_op jit(solution)/shard_map/pallas_call | solution.py:312
  116.3 1.6 %collective-permute-done.20.refs_8_ = bf16[4,272,256]{2,1,0:T(8,128)(2,1)S(1)} collective-permute-done((bf16[4,272,256]{2,1,0:T(8,128)(2,1)S(1)}, bf16[4,272,256]{2,1,0:T(8,128)(2,1)S(1)}, u32[]{:S(2)}, u32[]{:S(2)}) %collective-permute-start.20) | collective-permute-done | bytes 557088 | tf_op jit(solution)/shard_map/ppermute | solution.py:388
  117.9 1.6 %collective-permute-done.17.refs_7_ = bf16[4,272,256]{2,1,0:T(8,128)(2,1)S(1)} collective-permute-done((bf16[4,272,256]{2,1,0:T(8,128)(2,1)S(1)}, bf16[4,272,256]{2,1,0:T(8,128)(2,1)S(1)}, u32[]{:S(2)}, u32[]{:S(2)}) %collective-permute-start.17) | collective-permute-done | bytes 557088 | tf_op jit(solution)/shard_map/ppermute | solution.py:388
  119.5 1.6 %collective-permute-start.19 = (bf16[4,272,256]{2,1,0:T(8,128)(2,1)S(1)}, bf16[4,272,256]{2,1,0:T(8,128)(2,1)S(1)}, u32[]{:S(2)}, u32[]{:S(2)}) collective-permute-start(bf16[4,272,256]{2,1,0:T(8,128)(2,1)S(1)} %collective-permute-done.17.refs_7_), channel_id=1, source_target_pairs={{0,32},{1,97},{2,34},{3,99},{4,36},{5,101},{6,38},{7,103},{8,40},{... | collective-permute-start | bytes 1671176 | tf_op jit(solution)/shard_map/ppermute | solution.py:388
  121.1 5.1 %shard_map.63 = (f32[8,128]{1,0:T(8,128)}, f32[128,64,128]{2,1,0:T(8,128)S(1)}, f32[16,64,128]{2,1,0:T(8,128)S(1)}) custom-call(s32[3]{0:T(128)S(1)} %pad_add_fusion.refs_0_, f32[128]{0:T(128)S(1)} %bitcast_multiply_fusion.refs_1_.own_w, f32[128]{0:T(128)S(1)} %collective-permute-done.1.refs_2_, ...), custom_call_target="tpu_custom_call", output_to_operand_aliasing={{1}: (9, {}), {2}: (10, {})} | custom-call | flops 1200000000 | bytes 3000000 | tf_op jit(solution)/shard_map/pallas_call | solution.py:312
  126.3 0.1 collective-permute-start.22
  126.4 3.8 %collective-permute-done.19.refs_7_ = bf16[4,272,256]{2,1,0:T(8,128)(2,1)S(1)} collective-permute-done((bf16[4,272,256]{2,1,0:T(8,128)(2,1)S(1)}, bf16[4,272,256]{2,1,0:T(8,128)(2,1)S(1)}, u32[]{:S(2)}, u32[]{:S(2)}) %collective-permute-start.19) | collective-permute-done | bytes 557088 | tf_op jit(solution)/shard_map/ppermute | solution.py:388
  130.2 2.8 %shard_map.64 = (f32[8,128]{1,0:T(8,128)}, f32[128,64,128]{2,1,0:T(8,128)S(1)}) custom-call(s32[3]{0:T(128)S(1)} %pad_add_fusion.refs_0_, f32[128]{0:T(128)S(1)} %bitcast_multiply_fusion.refs_1_.own_w, f32[128]{0:T(128)S(1)} %collective-permute-done.1.refs_2_, bf16[272,256]{1,0:T(8,128)(2,1)S(1)} %get-tuple-element.54.refs_3_, ...), custom_call_target="tpu_custom_call", output_to_operand_aliasing={{1}: (8, {})} | custom-call | flops 400000000 | bytes 3000000 | tf_op jit(solution)/shard_map/pallas_call | solution.py:312
  133.1 3.9 %finish.1 = f32[8192,128]{1,0:T(8,128)} custom-call(s32[128]{0:T(128)S(1)} %and_select_fusion.8.src_ref, f32[128]{0:T(128)S(1)} %bitcast_multiply_fusion.refs_1_.own_w, f32[128,64,128]{2,1,0:T(8,128)S(1)} %get-tuple-element.100.own_ref, f32[48,64,128]{2,1,0:T(8,128)S(1)} %collective-permute-done.21.early_ref, f32[16,64,128]{2,1,0:T(8,128)S(1)} %collective-permute-done.22.late_ref), custom_call_target="tpu_custom_call" | custom-call | flops 1000000 | bytes 8000000 | tf_op jit(solution)/shard_map/finish/pallas_call | solution.py:362
  (20 shorter events, 0.1 us)
Async XLA Ops:
  1.0 1.0 copy-start
  2.0 0.9 copy-start.1
  3.5 7.3 %collective-permute-start.2 = (bf16[272,256]{1,0:T(8,128)(2,1)S(1)}, bf16[272,256]{1,0:T(8,128)(2,1)S(1)}, u32[]{:S(2)}, u32[]{:S(2)}) collective-permute-start(bf16[272,256]{1,0:T(8,128)(2,1)S(1)} %get-tuple-element.54.refs_3_), channel_id=1, source_target_pairs={{0,1},{1,0},{2,3},{3,2},{4,5},{5,4},{6,7},{7,6},{8,9},{9,8},{10,11... | collective-permute-start | bytes 417800 | tf_op jit(solution)/shard_map/ppermute | solution.py:388
  3.6 7.6 %collective-permute-start = (bf16[272,256]{1,0:T(8,128)(2,1)S(1)}, bf16[272,256]{1,0:T(8,128)(2,1)S(1)}, u32[]{:S(2)}, u32[]{:S(2)}) collective-permute-start(bf16[272,256]{1,0:T(8,128)(2,1)S(1)} %get-tuple-element.54.refs_3_), channel_id=1, source_target_pairs={{0,64},{1,65},{2,66},{3,67},{4,68},{5,69},{6,70},{7,71},{8,72},{9,... | collective-permute-start | bytes 417800 | tf_op jit(solution)/shard_map/ppermute | solution.py:388
  9.6 1.2 collective-permute-start.1
  11.2 1.4 collective-permute-start.3
  12.7 30.0 %collective-permute-start.4 = (bf16[4,272,256]{2,1,0:T(8,128)(2,1)S(1)}, bf16[4,272,256]{2,1,0:T(8,128)(2,1)S(1)}, u32[]{:S(2)}, u32[]{:S(2)}) collective-permute-start(bf16[4,272,256]{2,1,0:T(8,128)(2,1)S(1)} %pad_maximum_fusion.refs_7_), channel_id=1, source_target_pairs={{0,2},{1,31},{2,4},{3,1},{4,6},{5,3},{6,8},{7,5},{8,10},{9,7},{10,... | collective-permute-start | bytes 1671176 | tf_op jit(solution)/shard_map/ppermute | solution.py:388
  15.6 28.7 %collective-permute-start.6 = (bf16[4,272,256]{2,1,0:T(8,128)(2,1)S(1)}, bf16[4,272,256]{2,1,0:T(8,128)(2,1)S(1)}, u32[]{:S(2)}, u32[]{:S(2)}) collective-permute-start(bf16[4,272,256]{2,1,0:T(8,128)(2,1)S(1)} %pad_maximum_fusion.refs_7_), channel_id=1, source_target_pairs={{0,32},{1,97},{2,34},{3,99},{4,36},{5,101},{6,38},{7,103},{8,40},{... | collective-permute-start | bytes 1671176 | tf_op jit(solution)/shard_map/ppermute | solution.py:388
  42.7 10.7 %collective-permute-start.5 = (bf16[4,272,256]{2,1,0:T(8,128)(2,1)S(1)}, bf16[4,272,256]{2,1,0:T(8,128)(2,1)S(1)}, u32[]{:S(2)}, u32[]{:S(2)}) collective-permute-start(bf16[4,272,256]{2,1,0:T(8,128)(2,1)S(1)} %collective-permute-done.4.refs_7_), channel_id=1, source_target_pairs={{0,2},{1,31},{2,4},{3,1},{4,6},{5,3},{6,8},{7,5},{8,10},{9,7},{10,... | collective-permute-start | bytes 1671176 | tf_op jit(solution)/shard_map/ppermute | solution.py:388
  42.7 12.3 %collective-permute-start.8 = (bf16[4,272,256]{2,1,0:T(8,128)(2,1)S(1)}, bf16[4,272,256]{2,1,0:T(8,128)(2,1)S(1)}, u32[]{:S(2)}, u32[]{:S(2)}) collective-permute-start(bf16[4,272,256]{2,1,0:T(8,128)(2,1)S(1)} %collective-permute-done.4.refs_7_), channel_id=1, source_target_pairs={{0,32},{1,97},{2,34},{3,99},{4,36},{5,101},{6,38},{7,103},{8,40},{... | collective-permute-start | bytes 1671176 | tf_op jit(solution)/shard_map/ppermute | solution.py:388
  53.4 10.7 %collective-permute-start.7 = (bf16[4,272,256]{2,1,0:T(8,128)(2,1)S(1)}, bf16[4,272,256]{2,1,0:T(8,128)(2,1)S(1)}, u32[]{:S(2)}, u32[]{:S(2)}) collective-permute-start(bf16[4,272,256]{2,1,0:T(8,128)(2,1)S(1)} %collective-permute-done.5.refs_7_), channel_id=1, source_target_pairs={{0,2},{1,31},{2,4},{3,1},{4,6},{5,3},{6,8},{7,5},{8,10},{9,7},{10,... | collective-permute-start | bytes 1671176 | tf_op jit(solution)/shard_map/ppermute | solution.py:388
  53.4 12.3 %collective-permute-start.10 = (bf16[4,272,256]{2,1,0:T(8,128)(2,1)S(1)}, bf16[4,272,256]{2,1,0:T(8,128)(2,1)S(1)}, u32[]{:S(2)}, u32[]{:S(2)}) collective-permute-start(bf16[4,272,256]{2,1,0:T(8,128)(2,1)S(1)} %collective-permute-done.5.refs_7_), channel_id=1, source_target_pairs={{0,32},{1,97},{2,34},{3,99},{4,36},{5,101},{6,38},{7,103},{8,40},{... | collective-permute-start | bytes 1671176 | tf_op jit(solution)/shard_map/ppermute | solution.py:388
  64.2 10.7 %collective-permute-start.9 = (bf16[4,272,256]{2,1,0:T(8,128)(2,1)S(1)}, bf16[4,272,256]{2,1,0:T(8,128)(2,1)S(1)}, u32[]{:S(2)}, u32[]{:S(2)}) collective-permute-start(bf16[4,272,256]{2,1,0:T(8,128)(2,1)S(1)} %collective-permute-done.7.refs_7_), channel_id=1, source_target_pairs={{0,2},{1,31},{2,4},{3,1},{4,6},{5,3},{6,8},{7,5},{8,10},{9,7},{10,... | collective-permute-start | bytes 1671176 | tf_op jit(solution)/shard_map/ppermute | solution.py:388
  64.2 12.3 %collective-permute-start.12 = (bf16[4,272,256]{2,1,0:T(8,128)(2,1)S(1)}, bf16[4,272,256]{2,1,0:T(8,128)(2,1)S(1)}, u32[]{:S(2)}, u32[]{:S(2)}) collective-permute-start(bf16[4,272,256]{2,1,0:T(8,128)(2,1)S(1)} %collective-permute-done.7.refs_7_), channel_id=1, source_target_pairs={{0,32},{1,97},{2,34},{3,99},{4,36},{5,101},{6,38},{7,103},{8,40},{... | collective-permute-start | bytes 1671176 | tf_op jit(solution)/shard_map/ppermute | solution.py:388
  74.9 10.7 %collective-permute-start.11 = (bf16[4,272,256]{2,1,0:T(8,128)(2,1)S(1)}, bf16[4,272,256]{2,1,0:T(8,128)(2,1)S(1)}, u32[]{:S(2)}, u32[]{:S(2)}) collective-permute-start(bf16[4,272,256]{2,1,0:T(8,128)(2,1)S(1)} %collective-permute-done.9.refs_7_), channel_id=1, source_target_pairs={{0,2},{1,31},{2,4},{3,1},{4,6},{5,3},{6,8},{7,5},{8,10},{9,7},{10,... | collective-permute-start | bytes 1671176 | tf_op jit(solution)/shard_map/ppermute | solution.py:388
  74.9 12.3 %collective-permute-start.14 = (bf16[4,272,256]{2,1,0:T(8,128)(2,1)S(1)}, bf16[4,272,256]{2,1,0:T(8,128)(2,1)S(1)}, u32[]{:S(2)}, u32[]{:S(2)}) collective-permute-start(bf16[4,272,256]{2,1,0:T(8,128)(2,1)S(1)} %collective-permute-done.9.refs_7_), channel_id=1, source_target_pairs={{0,32},{1,97},{2,34},{3,99},{4,36},{5,101},{6,38},{7,103},{8,40},{... | collective-permute-start | bytes 1671176 | tf_op jit(solution)/shard_map/ppermute | solution.py:388
  85.7 10.7 %collective-permute-start.13 = (bf16[4,272,256]{2,1,0:T(8,128)(2,1)S(1)}, bf16[4,272,256]{2,1,0:T(8,128)(2,1)S(1)}, u32[]{:S(2)}, u32[]{:S(2)}) collective-permute-start(bf16[4,272,256]{2,1,0:T(8,128)(2,1)S(1)} %collective-permute-done.11.refs_7_), channel_id=1, source_target_pairs={{0,2},{1,31},{2,4},{3,1},{4,6},{5,3},{6,8},{7,5},{8,10},{9,7},{10,... | collective-permute-start | bytes 1671176 | tf_op jit(solution)/shard_map/ppermute | solution.py:388
  85.7 10.7 %collective-permute-start.16 = (bf16[4,272,256]{2,1,0:T(8,128)(2,1)S(1)}, bf16[4,272,256]{2,1,0:T(8,128)(2,1)S(1)}, u32[]{:S(2)}, u32[]{:S(2)}) collective-permute-start(bf16[4,272,256]{2,1,0:T(8,128)(2,1)S(1)} %collective-permute-done.11.refs_7_), channel_id=1, source_target_pairs={{0,32},{1,97},{2,34},{3,99},{4,36},{5,101},{6,38},{7,103},{8,40},{... | collective-permute-start | bytes 1671176 | tf_op jit(solution)/shard_map/ppermute | solution.py:388
  96.4 10.7 %collective-permute-start.15 = (bf16[4,272,256]{2,1,0:T(8,128)(2,1)S(1)}, bf16[4,272,256]{2,1,0:T(8,128)(2,1)S(1)}, u32[]{:S(2)}, u32[]{:S(2)}) collective-permute-start(bf16[4,272,256]{2,1,0:T(8,128)(2,1)S(1)} %collective-permute-done.13.refs_7_), channel_id=1, source_target_pairs={{0,2},{1,31},{2,4},{3,1},{4,6},{5,3},{6,8},{7,5},{8,10},{9,7},{10,... | collective-permute-start | bytes 1671176 | tf_op jit(solution)/shard_map/ppermute | solution.py:388
  100.9 32.2 %collective-permute-start.21 = (f32[48,64,128]{2,1,0:T(8,128)S(1)}, f32[48,64,128]{2,1,0:T(8,128)S(1)}, u32[]{:S(2)}, u32[]{:S(2)}) collective-permute-start(f32[48,64,128]{2,1,0:T(8,128)S(1)} %get-tuple-element.101), channel_id=1, source_target_pairs={{0,1},{1,0},{2,3},{3,2},{4,5},{5,4},{6,7},{7,6},{8,9},{9,8},{10,11... | collective-permute-start | bytes 4718600 | tf_op jit(solution)/shard_map/ppermute | solution.py:388
  101.0 10.9 %collective-permute-start.18 = (bf16[4,272,256]{2,1,0:T(8,128)(2,1)S(1)}, bf16[4,272,256]{2,1,0:T(8,128)(2,1)S(1)}, u32[]{:S(2)}, u32[]{:S(2)}) collective-permute-start(bf16[4,272,256]{2,1,0:T(8,128)(2,1)S(1)} %collective-permute-done.13.refs_7_), channel_id=1, source_target_pairs={{0,32},{1,97},{2,34},{3,99},{4,36},{5,101},{6,38},{7,103},{8,40},{... | collective-permute-start | bytes 1671176 | tf_op jit(solution)/shard_map/ppermute | solution.py:388
  107.2 10.7 %collective-permute-start.20 = (bf16[4,272,256]{2,1,0:T(8,128)(2,1)S(1)}, bf16[4,272,256]{2,1,0:T(8,128)(2,1)S(1)}, u32[]{:S(2)}, u32[]{:S(2)}) collective-permute-start(bf16[4,272,256]{2,1,0:T(8,128)(2,1)S(1)} %collective-permute-done.15.refs_7_), channel_id=1, source_target_pairs={{0,32},{1,97},{2,34},{3,99},{4,36},{5,101},{6,38},{7,103},{8,40},{... | collective-permute-start | bytes 1671176 | tf_op jit(solution)/shard_map/ppermute | solution.py:388
  108.7 10.7 %collective-permute-start.17 = (bf16[4,272,256]{2,1,0:T(8,128)(2,1)S(1)}, bf16[4,272,256]{2,1,0:T(8,128)(2,1)S(1)}, u32[]{:S(2)}, u32[]{:S(2)}) collective-permute-start(bf16[4,272,256]{2,1,0:T(8,128)(2,1)S(1)} %collective-permute-done.15.refs_7_), channel_id=1, source_target_pairs={{0,2},{1,31},{2,4},{3,1},{4,6},{5,3},{6,8},{7,5},{8,10},{9,7},{10,... | collective-permute-start | bytes 1671176 | tf_op jit(solution)/shard_map/ppermute | solution.py:388
  119.5 10.7 %collective-permute-start.19 = (bf16[4,272,256]{2,1,0:T(8,128)(2,1)S(1)}, bf16[4,272,256]{2,1,0:T(8,128)(2,1)S(1)}, u32[]{:S(2)}, u32[]{:S(2)}) collective-permute-start(bf16[4,272,256]{2,1,0:T(8,128)(2,1)S(1)} %collective-permute-done.17.refs_7_), channel_id=1, source_target_pairs={{0,32},{1,97},{2,34},{3,99},{4,36},{5,101},{6,38},{7,103},{8,40},{... | collective-permute-start | bytes 1671176 | tf_op jit(solution)/shard_map/ppermute | solution.py:388
  126.3 6.8 %collective-permute-start.22 = (f32[16,64,128]{2,1,0:T(8,128)S(1)}, f32[16,64,128]{2,1,0:T(8,128)S(1)}, u32[]{:S(2)}, u32[]{:S(2)}) collective-permute-start(f32[16,64,128]{2,1,0:T(8,128)S(1)} %get-tuple-element.102), channel_id=1, source_target_pairs={{0,1},{1,0},{2,3},{3,2},{4,5},{5,4},{6,7},{7,6},{8,9},{9,8},{10,11... | collective-permute-start | bytes 1572872 | tf_op jit(solution)/shard_map/ppermute | solution.py:388
where the time goes:
time: 137 us
  Pallas kernels  56.3 us (41%)
  waiting for transfers between devices  54.4 us (40%)
  starting transfers between devices  20.5 us (15%)
  local copies, waits for them, and re-layouts  4.18 us (3%)
    ppermute x23, waiting for transfers between devices, move(): return lax.ppermute(value, 'row', pairs)  54.4 us
    pallas_call x10, Pallas kernels, stage_call(): pl.pallas_call(body, out_shape=out_shape, in_specs=specs, out_specs=out_s...  51.9 us
    ppermute x23, starting transfers between devices, move(): return lax.ppermute(value, 'row', pairs)  20.5 us
    pallas_call x1, Pallas kernels, finish_call(): pl.pallas_call(finish_body, grid=(total // block,), out_shape=jax.ShapeDt...  3.92 us
  transfers between devices with their start and end apart: 23, of which 14 were waited for; matrix products, arithmetic and copies ran while one was open for 1% of the time, Pallas kernels for 38%

commit v1 on v0

--- a/solution.py
+++ b/solution.py
@@ -55,55 +55,42 @@
     return np.concatenate([first, wide, middle], axis=0), turn
 
 
-def fold_body(whole_ref, *refs):
-    many = (len(refs) - 2) // 2
-    sources, out_ref, copied, sems = refs[:many], refs[many], refs[many + 1 : -1], refs[-1]
-    copies = [
-        pltpu.make_async_copy(source, target, sems.at[n])
-        for n, (source, target) in enumerate(zip(sources, copied))
-    ]
-    for copy in copies:
-        copy.start()
+def fold_body(whole_ref, out_ref):
     rows, column = whole_ref.shape
     width = column // 2
-    half = rows // 2
     whole = whole_ref[...]
-    right = whole[:, width:]
     down = lax.broadcasted_iota(jnp.int32, (width, width), 0)
     over = lax.broadcasted_iota(jnp.int32, (width, width), 1)
     mirror = jnp.where(down == lax.rem(width - over, width), 1.0, 0.0).astype(jnp.bfloat16)
-    flipped = jnp.dot(right, mirror, preferred_element_type=jnp.float32).astype(jnp.bfloat16)
+    flipped = jnp.dot(whole[:, width:], mirror, preferred_element_type=jnp.float32)
     out_ref[pl.ds(0, rows), :] = whole[:, :width]
-    out_ref[pl.ds(rows, rows), :] = flipped
-    extra = out_ref.shape[0] - 2 * rows
-    over = lax.broadcasted_iota(jnp.int32, (extra, width), 1)
-    pick = jnp.where(over == 0, 1.0, 0.0).astype(jnp.bfloat16)
-    straight = lax.dot_general(
-        pick, right, (((1,), (1,)), ((), ())), preferred_element_type=jnp.float32
-    )
-    crossed = jnp.concatenate([straight[:, half:], -straight[:, :half]], axis=1)
-    out_ref[pl.ds(2 * rows, extra), :] = jnp.concatenate([straight, crossed], axis=1).astype(
-        jnp.bfloat16
-    )
-    for copy in copies:
-        copy.wait()
-
-
-def fold_call(whole, tables):
+    out_ref[pl.ds(rows, rows), :] = flipped.astype(jnp.bfloat16)
+
+
+def fold_call(whole):
     rows, column = whole.shape
-    vmem = pl.BlockSpec(memory_space=pltpu.VMEM)
-    hbm = pl.BlockSpec(memory_space=pltpu.HBM)
-    own = jax.ShapeDtypeStruct((2 * rows + 16, column // 2), jnp.bfloat16)
     return pl.pallas_call(
         fold_body,
-        out_shape=[own] + [jax.ShapeDtypeStruct(table.shape, table.dtype) for table in tables],
-        in_specs=[vmem] + [hbm] * len(tables),
-        out_specs=[vmem] * (1 + len(tables)),
-        scratch_shapes=[pltpu.SemaphoreType.DMA((len(tables),))],
+        out_shape=jax.ShapeDtypeStruct((2 * rows, column // 2), jnp.bfloat16),
+        in_specs=[pl.BlockSpec(memory_space=pltpu.VMEM)],
+        out_specs=pl.BlockSpec(memory_space=pltpu.VMEM),
         cost_estimate=pl.CostEstimate(flops=1_000_000, bytes_accessed=300_000, transcendentals=0),
         compiler_params=pltpu.CompilerParams(vmem_limit_bytes=16 * 1024 * 1024),
         name="fold",
-    )(whole, *tables)
+    )(whole)
+
+
+def first_column(block):
+    over = lax.broadcasted_iota(jnp.int32, (16, block.shape[1]), 1)
+    pick = jnp.where(over == 0, 1.0, 0.0).astype(jnp.bfloat16)
+    return lax.dot_general(
+        pick, block, (((1,), (1,)), ((), ())), preferred_element_type=jnp.float32
+    )
+
+
+def swap_halves(value):
+    half = value.shape[1] // 2
+    return jnp.concatenate([value[:, half:], value[:, :half]], axis=1)
 
 
 def split(value):
@@ -176,19 +163,19 @@
     lane = lax.broadcasted_iota(jnp.int32, (2 * per, INNER), 1)
     spot = lax.broadcasted_iota(jnp.int32, (2 * per, INNER), 0)
     straight = jnp.zeros((2 * per, INNER), jnp.float32)
-    crossed = jnp.zeros((2 * per, INNER), jnp.float32)
     for side, (present, rows) in enumerate(plan):
         for e in range(side * per, (side + 1) * per if present else 0):
-            edge = held[e, size:].astype(jnp.float32)[: 2 * per]
-            straight = jnp.where(spot == e, edge[:, :INNER], straight)
-            crossed = jnp.where(spot == e, edge[:, INNER:], crossed)
+            edge = first_column(held[e, 2 * quarter :])[: 2 * per]
+            straight = jnp.where(spot == e, edge, straight)
+    crossed = jnp.where(lane < INNER // 2, 1.0, -1.0) * swap_halves(straight)
     parts = []
     for row in range(2):
         mine = mine1 if row else mine0
-        wide[row] = mine[:size].astype(jnp.float32) * weight
-        edge = mine[size:].astype(jnp.float32)[: 2 * per]
-        real = jnp.where(lane < INNER // 2, edge[:, :INNER], -edge[:, INNER:])
-        imag = jnp.where(lane < INNER // 2, edge[:, INNER:], edge[:, :INNER])
+        wide[row] = mine[...].astype(jnp.float32) * weight
+        edge = first_column(mine[2 * quarter :])[: 2 * per]
+        other = swap_halves(edge)
+        real = jnp.where(lane < INNER // 2, edge, other)
+        imag = jnp.where(lane < INNER // 2, other, edge)
         parts.append(real * straight + imag * crossed)
     high, low = split(jnp.concatenate(parts, axis=0))
     rows_of = high.shape[0]
@@ -207,7 +194,7 @@
         return pltpu.make_async_copy(result_ref.at[code], to, sems.at[code])
 
     def columns(code):
-        other = held[code // 2, :size].astype(jnp.float32)
+        other = held[code // 2].astype(jnp.float32)
         return turned_columns(*split(cross_spectrum(other, wide[code % 2])), table, turn)
 
     def middle_of(code):
@@ -400,7 +387,7 @@
     x, z, c = me // (along * CORES), me // CORES % along, me % CORES
     info = jnp.stack([x, z, c]).astype(jnp.int32)
 
-    own, *tables = fold_call(spectra.reshape(2 * freq // column, column), tables)
+    own = fold_call(spectra.reshape(2 * freq // column, column))
     across = move(own, lambda x, z, c: (x + 2 - 4 * c, z, c))
     flag = lax.dynamic_slice_in_dim(available, me, 1, 0).astype(jnp.float32)
     own_w = pair_mask[0].astype(jnp.float32) * flag * available.astype(jnp.float32)

time: 137 us -> 133 us (0.971)
  waiting for transfers between devices: 54.4 us -> 47.8 us
  Pallas kernels: 56.3 us -> 59.3 us
    ppermute x23, waiting for transfers between devices: 54.4 us -> 47.8 us  [move(): return lax.ppermute(value, 'row', pairs)]
    pallas_call x10, Pallas kernels: 51.9 us -> 55.3 us  [stage_call(): pl.pallas_call(body, out_shape=out_shape, in_specs=specs, out_specs=out_s...]
  transfers between devices with their start and end apart: 23 -> 23, of which waited for: 14 -> 15; matrix products, arithmetic and copies ran while one was open for 1% -> 2% of each run, Pallas kernels for 38% -> 41%
where the time goes in v1:
time: 133 us
  Pallas kernels  59.3 us (45%)
  waiting for transfers between devices  47.8 us (36%)
  starting transfers between devices  20.3 us (15%)
  local copies, waits for them, and re-layouts  4.18 us (3%)
    pallas_call x10, Pallas kernels, stage_call(): pl.pallas_call(body, out_shape=out_shape, in_specs=specs, out_specs=out_s...  55.3 us
    ppermute x23, waiting for transfers between devices, move(): return lax.ppermute(value, 'row', pairs)  47.8 us
    ppermute x23, starting transfers between devices, move(): return lax.ppermute(value, 'row', pairs)  20.3 us
    pallas_call x1, Pallas kernels, finish_call(): pl.pallas_call(finish_body, grid=(total // block,), out_shape=jax.ShapeDt...  3.92 us
  transfers between devices with their start and end apart: 23, of which 15 were waited for; matrix products, arithmetic and copies ran while one was open for 2% of the time, Pallas kernels for 41%

profile of v1, /device:TPU:40, one launch (start us, length us, event | category | flops | bytes accessed | tf_op | source)
XLA Modules:
  0.0 133.2 jit_solution(6679436204528714486)
XLA Ops:
  0.0 1.0 reshape.12.whole_ref
  1.0 0.2 fold.1.refs_3_
  1.1 0.1 collective-permute-start.2
  1.3 3.4 %collective-permute-start = (bf16[256,256]{1,0:T(8,128)(2,1)S(1)}, bf16[256,256]{1,0:T(8,128)(2,1)S(1)}, u32[]{:S(2)}, u32[]{:S(2)}) collective-permute-start(bf16[256,256]{1,0:T(8,128)(2,1)S(1)} %fold.1.refs_3_), channel_id=1, source_target_pairs={{0,64},{1,65},{2,66},{3,67},{4,68},{5,69},{6,70},{7,71},{8,72},{9,... | collective-permute-start | bytes 393224 | tf_op jit(solution)/shard_map/ppermute | solution.py:375
  4.7 1.2 dynamic_slice.3
  6.6 0.7 bitcast_multiply_fusion.refs_1_.own_w
  7.3 0.1 collective-permute-start.1
  7.4 0.1 pad_add_fusion.refs_0_
  7.4 1.0 collective-permute-done.1.refs_2_
  8.5 0.3 collective-permute-done
  8.7 1.3 %collective-permute-done.3 = bf16[256,256]{1,0:T(8,128)(2,1)S(1)} collective-permute-done((bf16[256,256]{1,0:T(8,128)(2,1)S(1)}, bf16[256,256]{1,0:T(8,128)(2,1)S(1)}, u32[]{:S(2)}, u32[]{:S(2)}) %collective-permute-start.3) | collective-permute-done | bytes 131104 | tf_op jit(solution)/shard_map/ppermute | solution.py:375
  10.2 2.9 %collective-permute-start.4 = (bf16[4,256,256]{2,1,0:T(8,128)(2,1)S(1)}, bf16[4,256,256]{2,1,0:T(8,128)(2,1)S(1)}, u32[]{:S(2)}, u32[]{:S(2)}) collective-permute-start(bf16[4,256,256]{2,1,0:T(8,128)(2,1)S(1)} %pad_maximum_fusion.refs_7_), channel_id=1, source_target_pairs={{0,2},{1,31},{2,4},{3,1},{4,6},{5,3},{6,8},{7,5},{8,10},{9,7},{10,... | collective-permute-start | bytes 1572872 | tf_op jit(solution)/shard_map/ppermute | solution.py:375
  13.0 1.6 %collective-permute-start.6 = (bf16[4,256,256]{2,1,0:T(8,128)(2,1)S(1)}, bf16[4,256,256]{2,1,0:T(8,128)(2,1)S(1)}, u32[]{:S(2)}, u32[]{:S(2)}) collective-permute-start(bf16[4,256,256]{2,1,0:T(8,128)(2,1)S(1)} %pad_maximum_fusion.refs_7_), channel_id=1, source_target_pairs={{0,32},{1,97},{2,34},{3,99},{4,36},{5,101},{6,38},{7,103},{8,40},{... | collective-permute-start | bytes 1572872 | tf_op jit(solution)/shard_map/ppermute | solution.py:375
  14.6 1.0 copy-done
  15.6 0.9 copy-done.1
  16.6 3.8 %shard_map.55 = (f32[8,128]{1,0:T(8,128)}, f32[128,64,128]{2,1,0:T(8,128)S(1)}) custom-call(s32[3]{0:T(128)S(1)} %pad_add_fusion.refs_0_, f32[128]{0:T(128)S(1)} %bitcast_multiply_fusion.refs_1_.own_w, f32[128]{0:T(128)S(1)} %collective-permute-done.1.refs_2_, bf16[256,256]{1,0:T(8,128)(2,1)S(1)} %fold.1.refs_3_, ...), custom_call_target="tpu_custom_call" | custom-call | flops 400000000 | bytes 3000000 | tf_op jit(solution)/shard_map/pallas_call | solution.py:299
  20.4 19.4 %collective-permute-done.4.refs_7_ = bf16[4,256,256]{2,1,0:T(8,128)(2,1)S(1)} collective-permute-done((bf16[4,256,256]{2,1,0:T(8,128)(2,1)S(1)}, bf16[4,256,256]{2,1,0:T(8,128)(2,1)S(1)}, u32[]{:S(2)}, u32[]{:S(2)}) %collective-permute-start.4) | collective-permute-done | bytes 524320 | tf_op jit(solution)/shard_map/ppermute | solution.py:375
  39.8 1.6 %collective-permute-start.8 = (bf16[4,256,256]{2,1,0:T(8,128)(2,1)S(1)}, bf16[4,256,256]{2,1,0:T(8,128)(2,1)S(1)}, u32[]{:S(2)}, u32[]{:S(2)}) collective-permute-start(bf16[4,256,256]{2,1,0:T(8,128)(2,1)S(1)} %collective-permute-done.4.refs_7_), channel_id=1, source_target_pairs={{0,32},{1,97},{2,34},{3,99},{4,36},{5,101},{6,38},{7,103},{8,40},{... | collective-permute-start | bytes 1572872 | tf_op jit(solution)/shard_map/ppermute | solution.py:375
  41.4 5.4 %shard_map.56 = (f32[8,128]{1,0:T(8,128)}, f32[128,64,128]{2,1,0:T(8,128)S(1)}, f32[48,64,128]{2,1,0:T(8,128)S(1)}) custom-call(s32[3]{0:T(128)S(1)} %pad_add_fusion.refs_0_, f32[128]{0:T(128)S(1)} %bitcast_multiply_fusion.refs_1_.own_w, f32[128]{0:T(128)S(1)} %collective-permute-done.1.refs_2_, ...), custom_call_target="tpu_custom_call", output_to_operand_aliasing={{1}: (9, {})} | custom-call | flops 1200000000 | bytes 3000000 | tf_op jit(solution)/shard_map/pallas_call | solution.py:299
  46.9 3.4 %collective-permute-done.5.refs_7_ = bf16[4,256,256]{2,1,0:T(8,128)(2,1)S(1)} collective-permute-done((bf16[4,256,256]{2,1,0:T(8,128)(2,1)S(1)}, bf16[4,256,256]{2,1,0:T(8,128)(2,1)S(1)}, u32[]{:S(2)}, u32[]{:S(2)}) %collective-permute-start.5) | collective-permute-done | bytes 524320 | tf_op jit(solution)/shard_map/ppermute | solution.py:375
  50.2 1.6 %collective-permute-start.10 = (bf16[4,256,256]{2,1,0:T(8,128)(2,1)S(1)}, bf16[4,256,256]{2,1,0:T(8,128)(2,1)S(1)}, u32[]{:S(2)}, u32[]{:S(2)}) collective-permute-start(bf16[4,256,256]{2,1,0:T(8,128)(2,1)S(1)} %collective-permute-done.5.refs_7_), channel_id=1, source_target_pairs={{0,32},{1,97},{2,34},{3,99},{4,36},{5,101},{6,38},{7,103},{8,40},{... | collective-permute-start | bytes 1572872 | tf_op jit(solution)/shard_map/ppermute | solution.py:375
  51.8 6.2 %shard_map.57 = (f32[8,128]{1,0:T(8,128)}, f32[128,64,128]{2,1,0:T(8,128)S(1)}, f32[48,64,128]{2,1,0:T(8,128)S(1)}) custom-call(s32[3]{0:T(128)S(1)} %pad_add_fusion.refs_0_, f32[128]{0:T(128)S(1)} %bitcast_multiply_fusion.refs_1_.own_w, f32[128]{0:T(128)S(1)} %collective-permute-done.1.refs_2_, ...), custom_call_target="tpu_custom_call", output_to_operand_aliasing={{1}: (9, {}), {2}: (10, {})} | custom-call | flops 1600000000 | bytes 3000000 | tf_op jit(solution)/shard_map/pallas_call | solution.py:299
  58.0 2.6 %collective-permute-done.7.refs_7_ = bf16[4,256,256]{2,1,0:T(8,128)(2,1)S(1)} collective-permute-done((bf16[4,256,256]{2,1,0:T(8,128)(2,1)S(1)}, bf16[4,256,256]{2,1,0:T(8,128)(2,1)S(1)}, u32[]{:S(2)}, u32[]{:S(2)}) %collective-permute-start.7) | collective-permute-done | bytes 524320 | tf_op jit(solution)/shard_map/ppermute | solution.py:375
  60.6 1.6 %collective-permute-start.12 = (bf16[4,256,256]{2,1,0:T(8,128)(2,1)S(1)}, bf16[4,256,256]{2,1,0:T(8,128)(2,1)S(1)}, u32[]{:S(2)}, u32[]{:S(2)}) collective-permute-start(bf16[4,256,256]{2,1,0:T(8,128)(2,1)S(1)} %collective-permute-done.7.refs_7_), channel_id=1, source_target_pairs={{0,32},{1,97},{2,34},{3,99},{4,36},{5,101},{6,38},{7,103},{8,40},{... | collective-permute-start | bytes 1572872 | tf_op jit(solution)/shard_map/ppermute | solution.py:375
  62.2 7.8 %shard_map.58 = (f32[8,128]{1,0:T(8,128)}, f32[128,64,128]{2,1,0:T(8,128)S(1)}, f32[48,64,128]{2,1,0:T(8,128)S(1)}) custom-call(s32[3]{0:T(128)S(1)} %pad_add_fusion.refs_0_, f32[128]{0:T(128)S(1)} %bitcast_multiply_fusion.refs_1_.own_w, f32[128]{0:T(128)S(1)} %collective-permute-done.1.refs_2_, ...), custom_call_target="tpu_custom_call", output_to_operand_aliasing={{1}: (9, {}), {2}: (10, {})} | custom-call | flops 1600000000 | bytes 3000000 | tf_op jit(solution)/shard_map/pallas_call | solution.py:299
  70.0 1.0 collective-permute-done.9.refs_7_
  71.0 1.6 %collective-permute-start.14 = (bf16[4,256,256]{2,1,0:T(8,128)(2,1)S(1)}, bf16[4,256,256]{2,1,0:T(8,128)(2,1)S(1)}, u32[]{:S(2)}, u32[]{:S(2)}) collective-permute-start(bf16[4,256,256]{2,1,0:T(8,128)(2,1)S(1)} %collective-permute-done.9.refs_7_), channel_id=1, source_target_pairs={{0,32},{1,97},{2,34},{3,99},{4,36},{5,101},{6,38},{7,103},{8,40},{... | collective-permute-start | bytes 1572872 | tf_op jit(solution)/shard_map/ppermute | solution.py:375
  72.6 6.9 %shard_map.59 = (f32[8,128]{1,0:T(8,128)}, f32[128,64,128]{2,1,0:T(8,128)S(1)}, f32[48,64,128]{2,1,0:T(8,128)S(1)}) custom-call(s32[3]{0:T(128)S(1)} %pad_add_fusion.refs_0_, f32[128]{0:T(128)S(1)} %bitcast_multiply_fusion.refs_1_.own_w, f32[128]{0:T(128)S(1)} %collective-permute-done.1.refs_2_, ...), custom_call_target="tpu_custom_call", output_to_operand_aliasing={{1}: (9, {}), {2}: (10, {})} | custom-call | flops 1600000000 | bytes 3000000 | tf_op jit(solution)/shard_map/pallas_call | solution.py:299
  79.5 1.9 %collective-permute-done.11.refs_7_ = bf16[4,256,256]{2,1,0:T(8,128)(2,1)S(1)} collective-permute-done((bf16[4,256,256]{2,1,0:T(8,128)(2,1)S(1)}, bf16[4,256,256]{2,1,0:T(8,128)(2,1)S(1)}, u32[]{:S(2)}, u32[]{:S(2)}) %collective-permute-start.11) | collective-permute-done | bytes 524320 | tf_op jit(solution)/shard_map/ppermute | solution.py:375
  81.4 1.6 %collective-permute-start.16 = (bf16[4,256,256]{2,1,0:T(8,128)(2,1)S(1)}, bf16[4,256,256]{2,1,0:T(8,128)(2,1)S(1)}, u32[]{:S(2)}, u32[]{:S(2)}) collective-permute-start(bf16[4,256,256]{2,1,0:T(8,128)(2,1)S(1)} %collective-permute-done.11.refs_7_), channel_id=1, source_target_pairs={{0,32},{1,97},{2,34},{3,99},{4,36},{5,101},{6,38},{7,103},{8,40},{... | collective-permute-start | bytes 1572872 | tf_op jit(solution)/shard_map/ppermute | solution.py:375
  83.0 7.0 %shard_map.60 = (f32[8,128]{1,0:T(8,128)}, f32[128,64,128]{2,1,0:T(8,128)S(1)}, f32[48,64,128]{2,1,0:T(8,128)S(1)}) custom-call(s32[3]{0:T(128)S(1)} %pad_add_fusion.refs_0_, f32[128]{0:T(128)S(1)} %bitcast_multiply_fusion.refs_1_.own_w, f32[128]{0:T(128)S(1)} %collective-permute-done.1.refs_2_, ...), custom_call_target="tpu_custom_call", output_to_operand_aliasing={{1}: (9, {}), {2}: (10, {})} | custom-call | flops 1600000000 | bytes 3000000 | tf_op jit(solution)/shard_map/pallas_call | solution.py:299
  90.0 1.8 %collective-permute-done.16.refs_8_ = bf16[4,256,256]{2,1,0:T(8,128)(2,1)S(1)} collective-permute-done((bf16[4,256,256]{2,1,0:T(8,128)(2,1)S(1)}, bf16[4,256,256]{2,1,0:T(8,128)(2,1)S(1)}, u32[]{:S(2)}, u32[]{:S(2)}) %collective-permute-start.16) | collective-permute-done | bytes 524320 | tf_op jit(solution)/shard_map/ppermute | solution.py:375
  91.8 1.6 %collective-permute-done.13.refs_7_ = bf16[4,256,256]{2,1,0:T(8,128)(2,1)S(1)} collective-permute-done((bf16[4,256,256]{2,1,0:T(8,128)(2,1)S(1)}, bf16[4,256,256]{2,1,0:T(8,128)(2,1)S(1)}, u32[]{:S(2)}, u32[]{:S(2)}) %collective-permute-start.13) | collective-permute-done | bytes 524320 | tf_op jit(solution)/shard_map/ppermute | solution.py:375
  93.4 4.8 %shard_map.61 = (f32[8,128]{1,0:T(8,128)}, f32[128,64,128]{2,1,0:T(8,128)S(1)}, f32[48,64,128]{2,1,0:T(8,128)S(1)}) custom-call(s32[3]{0:T(128)S(1)} %pad_add_fusion.refs_0_, f32[128]{0:T(128)S(1)} %bitcast_multiply_fusion.refs_1_.own_w, f32[128]{0:T(128)S(1)} %collective-permute-done.1.refs_2_, ...), custom_call_target="tpu_custom_call", output_to_operand_aliasing={{1}: (9, {}), {2}: (10, {})} | custom-call | flops 1600000000 | bytes 3000000 | tf_op jit(solution)/shard_map/pallas_call | solution.py:299
  98.2 0.1 collective-permute-start.21
  98.3 1.0 collective-permute-start.18
  99.3 4.5 %collective-permute-done.15.refs_7_ = bf16[4,256,256]{2,1,0:T(8,128)(2,1)S(1)} collective-permute-done((bf16[4,256,256]{2,1,0:T(8,128)(2,1)S(1)}, bf16[4,256,256]{2,1,0:T(8,128)(2,1)S(1)}, u32[]{:S(2)}, u32[]{:S(2)}) %collective-permute-start.15) | collective-permute-done | bytes 524320 | tf_op jit(solution)/shard_map/ppermute | solution.py:375
  103.8 1.6 %collective-permute-start.20 = (bf16[4,256,256]{2,1,0:T(8,128)(2,1)S(1)}, bf16[4,256,256]{2,1,0:T(8,128)(2,1)S(1)}, u32[]{:S(2)}, u32[]{:S(2)}) collective-permute-start(bf16[4,256,256]{2,1,0:T(8,128)(2,1)S(1)} %collective-permute-done.15.refs_7_), channel_id=1, source_target_pairs={{0,32},{1,97},{2,34},{3,99},{4,36},{5,101},{6,38},{7,103},{8,40},{... | collective-permute-start | bytes 1572872 | tf_op jit(solution)/shard_map/ppermute | solution.py:375
  105.4 3.4 %collective-permute-done.18.refs_8_ = bf16[4,256,256]{2,1,0:T(8,128)(2,1)S(1)} collective-permute-done((bf16[4,256,256]{2,1,0:T(8,128)(2,1)S(1)}, bf16[4,256,256]{2,1,0:T(8,128)(2,1)S(1)}, u32[]{:S(2)}, u32[]{:S(2)}) %collective-permute-start.18) | collective-permute-done | bytes 524320 | tf_op jit(solution)/shard_map/ppermute | solution.py:375
  108.8 4.8 %shard_map.62 = (f32[8,128]{1,0:T(8,128)}, f32[128,64,128]{2,1,0:T(8,128)S(1)}, f32[16,64,128]{2,1,0:T(8,128)S(1)}) custom-call(s32[3]{0:T(128)S(1)} %pad_add_fusion.refs_0_, f32[128]{0:T(128)S(1)} %bitcast_multiply_fusion.refs_1_.own_w, f32[128]{0:T(128)S(1)} %collective-permute-done.1.refs_2_, ...), custom_call_target="tpu_custom_call", output_to_operand_aliasing={{1}: (9, {})} | custom-call | flops 1600000000 | bytes 3000000 | tf_op jit(solution)/shard_map/pallas_call | solution.py:299
  113.6 0.8 collective-permute-done.20.refs_8_
  114.4 1.4 %collective-permute-done.17.refs_7_ = bf16[4,256,256]{2,1,0:T(8,128)(2,1)S(1)} collective-permute-done((bf16[4,256,256]{2,1,0:T(8,128)(2,1)S(1)}, bf16[4,256,256]{2,1,0:T(8,128)(2,1)S(1)}, u32[]{:S(2)}, u32[]{:S(2)}) %collective-permute-start.17) | collective-permute-done | bytes 524320 | tf_op jit(solution)/shard_map/ppermute | solution.py:375
  115.8 1.3 %collective-permute-start.19 = (bf16[4,256,256]{2,1,0:T(8,128)(2,1)S(1)}, bf16[4,256,256]{2,1,0:T(8,128)(2,1)S(1)}, u32[]{:S(2)}, u32[]{:S(2)}) collective-permute-start(bf16[4,256,256]{2,1,0:T(8,128)(2,1)S(1)} %collective-permute-done.17.refs_7_), channel_id=1, source_target_pairs={{0,32},{1,97},{2,34},{3,99},{4,36},{5,101},{6,38},{7,103},{8,40},{... | collective-permute-start | bytes 1572872 | tf_op jit(solution)/shard_map/ppermute | solution.py:375
  117.1 5.5 %shard_map.63 = (f32[8,128]{1,0:T(8,128)}, f32[128,64,128]{2,1,0:T(8,128)S(1)}, f32[16,64,128]{2,1,0:T(8,128)S(1)}) custom-call(s32[3]{0:T(128)S(1)} %pad_add_fusion.refs_0_, f32[128]{0:T(128)S(1)} %bitcast_multiply_fusion.refs_1_.own_w, f32[128]{0:T(128)S(1)} %collective-permute-done.1.refs_2_, ...), custom_call_target="tpu_custom_call", output_to_operand_aliasing={{1}: (9, {}), {2}: (10, {})} | custom-call | flops 1200000000 | bytes 3000000 | tf_op jit(solution)/shard_map/pallas_call | solution.py:299
  122.6 0.1 collective-permute-start.22
  122.8 3.4 %collective-permute-done.19.refs_7_ = bf16[4,256,256]{2,1,0:T(8,128)(2,1)S(1)} collective-permute-done((bf16[4,256,256]{2,1,0:T(8,128)(2,1)S(1)}, bf16[4,256,256]{2,1,0:T(8,128)(2,1)S(1)}, u32[]{:S(2)}, u32[]{:S(2)}) %collective-permute-start.19) | collective-permute-done | bytes 524320 | tf_op jit(solution)/shard_map/ppermute | solution.py:375
  126.2 3.1 %shard_map.64 = (f32[8,128]{1,0:T(8,128)}, f32[128,64,128]{2,1,0:T(8,128)S(1)}) custom-call(s32[3]{0:T(128)S(1)} %pad_add_fusion.refs_0_, f32[128]{0:T(128)S(1)} %bitcast_multiply_fusion.refs_1_.own_w, f32[128]{0:T(128)S(1)} %collective-permute-done.1.refs_2_, bf16[256,256]{1,0:T(8,128)(2,1)S(1)} %fold.1.refs_3_, ...), custom_call_target="tpu_custom_call", output_to_operand_aliasing={{1}: (8, {})} | custom-call | flops 400000000 | bytes 3000000 | tf_op jit(solution)/shard_map/pallas_call | solution.py:299
  129.3 3.9 %finish.1 = f32[8192,128]{1,0:T(8,128)} custom-call(s32[128]{0:T(128)S(1)} %and_select_fusion.8.src_ref, f32[128]{0:T(128)S(1)} %bitcast_multiply_fusion.refs_1_.own_w, f32[128,64,128]{2,1,0:T(8,128)S(1)} %get-tuple-element.94.own_ref, f32[48,64,128]{2,1,0:T(8,128)S(1)} %collective-permute-done.21.early_ref, f32[16,64,128]{2,1,0:T(8,128)S(1)} %collective-permute-done.22.late_ref), custom_call_target="tpu_custom_call" | custom-call | flops 1000000 | bytes 8000000 | tf_op jit(solution)/shard_map/finish/pallas_call | solution.py:349
  (20 shorter events, 0.1 us)
Async XLA Ops:
  1.1 7.3 %collective-permute-start.2 = (bf16[256,256]{1,0:T(8,128)(2,1)S(1)}, bf16[256,256]{1,0:T(8,128)(2,1)S(1)}, u32[]{:S(2)}, u32[]{:S(2)}) collective-permute-start(bf16[256,256]{1,0:T(8,128)(2,1)S(1)} %fold.1.refs_3_), channel_id=1, source_target_pairs={{0,1},{1,0},{2,3},{3,2},{4,5},{5,4},{6,7},{7,6},{8,9},{9,8},{10,11... | collective-permute-start | bytes 393224 | tf_op jit(solution)/shard_map/ppermute | solution.py:375
  1.3 7.4 %collective-permute-start = (bf16[256,256]{1,0:T(8,128)(2,1)S(1)}, bf16[256,256]{1,0:T(8,128)(2,1)S(1)}, u32[]{:S(2)}, u32[]{:S(2)}) collective-permute-start(bf16[256,256]{1,0:T(8,128)(2,1)S(1)} %fold.1.refs_3_), channel_id=1, source_target_pairs={{0,64},{1,65},{2,66},{3,67},{4,68},{5,69},{6,70},{7,71},{8,72},{9,... | collective-permute-start | bytes 393224 | tf_op jit(solution)/shard_map/ppermute | solution.py:375
  7.3 1.2 collective-permute-start.1
  8.7 1.3 %collective-permute-start.3 = (bf16[256,256]{1,0:T(8,128)(2,1)S(1)}, bf16[256,256]{1,0:T(8,128)(2,1)S(1)}, u32[]{:S(2)}, u32[]{:S(2)}) collective-permute-start(bf16[256,256]{1,0:T(8,128)(2,1)S(1)} %collective-permute-done), channel_id=1, source_target_pairs={{0,1},{1,0},{2,3},{3,2},{4,5},{5,4},{6,7},{7,6},{8,9},{9,8},{10,11... | collective-permute-start | bytes 393224 | tf_op jit(solution)/shard_map/ppermute | solution.py:375
  10.2 29.7 %collective-permute-start.4 = (bf16[4,256,256]{2,1,0:T(8,128)(2,1)S(1)}, bf16[4,256,256]{2,1,0:T(8,128)(2,1)S(1)}, u32[]{:S(2)}, u32[]{:S(2)}) collective-permute-start(bf16[4,256,256]{2,1,0:T(8,128)(2,1)S(1)} %pad_maximum_fusion.refs_7_), channel_id=1, source_target_pairs={{0,2},{1,31},{2,4},{3,1},{4,6},{5,3},{6,8},{7,5},{8,10},{9,7},{10,... | collective-permute-start | bytes 1572872 | tf_op jit(solution)/shard_map/ppermute | solution.py:375
  13.0 28.4 %collective-permute-start.6 = (bf16[4,256,256]{2,1,0:T(8,128)(2,1)S(1)}, bf16[4,256,256]{2,1,0:T(8,128)(2,1)S(1)}, u32[]{:S(2)}, u32[]{:S(2)}) collective-permute-start(bf16[4,256,256]{2,1,0:T(8,128)(2,1)S(1)} %pad_maximum_fusion.refs_7_), channel_id=1, source_target_pairs={{0,32},{1,97},{2,34},{3,99},{4,36},{5,101},{6,38},{7,103},{8,40},{... | collective-permute-start | bytes 1572872 | tf_op jit(solution)/shard_map/ppermute | solution.py:375
  14.6 1.0 copy-start
  15.6 0.9 copy-start.1
  39.8 10.4 %collective-permute-start.5 = (bf16[4,256,256]{2,1,0:T(8,128)(2,1)S(1)}, bf16[4,256,256]{2,1,0:T(8,128)(2,1)S(1)}, u32[]{:S(2)}, u32[]{:S(2)}) collective-permute-start(bf16[4,256,256]{2,1,0:T(8,128)(2,1)S(1)} %collective-permute-done.4.refs_7_), channel_id=1, source_target_pairs={{0,2},{1,31},{2,4},{3,1},{4,6},{5,3},{6,8},{7,5},{8,10},{9,7},{10,... | collective-permute-start | bytes 1572872 | tf_op jit(solution)/shard_map/ppermute | solution.py:375
  39.8 12.0 %collective-permute-start.8 = (bf16[4,256,256]{2,1,0:T(8,128)(2,1)S(1)}, bf16[4,256,256]{2,1,0:T(8,128)(2,1)S(1)}, u32[]{:S(2)}, u32[]{:S(2)}) collective-permute-start(bf16[4,256,256]{2,1,0:T(8,128)(2,1)S(1)} %collective-permute-done.4.refs_7_), channel_id=1, source_target_pairs={{0,32},{1,97},{2,34},{3,99},{4,36},{5,101},{6,38},{7,103},{8,40},{... | collective-permute-start | bytes 1572872 | tf_op jit(solution)/shard_map/ppermute | solution.py:375
  50.2 10.4 %collective-permute-start.7 = (bf16[4,256,256]{2,1,0:T(8,128)(2,1)S(1)}, bf16[4,256,256]{2,1,0:T(8,128)(2,1)S(1)}, u32[]{:S(2)}, u32[]{:S(2)}) collective-permute-start(bf16[4,256,256]{2,1,0:T(8,128)(2,1)S(1)} %collective-permute-done.5.refs_7_), channel_id=1, source_target_pairs={{0,2},{1,31},{2,4},{3,1},{4,6},{5,3},{6,8},{7,5},{8,10},{9,7},{10,... | collective-permute-start | bytes 1572872 | tf_op jit(solution)/shard_map/ppermute | solution.py:375
  50.2 12.0 %collective-permute-start.10 = (bf16[4,256,256]{2,1,0:T(8,128)(2,1)S(1)}, bf16[4,256,256]{2,1,0:T(8,128)(2,1)S(1)}, u32[]{:S(2)}, u32[]{:S(2)}) collective-permute-start(bf16[4,256,256]{2,1,0:T(8,128)(2,1)S(1)} %collective-permute-done.5.refs_7_), channel_id=1, source_target_pairs={{0,32},{1,97},{2,34},{3,99},{4,36},{5,101},{6,38},{7,103},{8,40},{... | collective-permute-start | bytes 1572872 | tf_op jit(solution)/shard_map/ppermute | solution.py:375
  60.6 10.4 %collective-permute-start.9 = (bf16[4,256,256]{2,1,0:T(8,128)(2,1)S(1)}, bf16[4,256,256]{2,1,0:T(8,128)(2,1)S(1)}, u32[]{:S(2)}, u32[]{:S(2)}) collective-permute-start(bf16[4,256,256]{2,1,0:T(8,128)(2,1)S(1)} %collective-permute-done.7.refs_7_), channel_id=1, source_target_pairs={{0,2},{1,31},{2,4},{3,1},{4,6},{5,3},{6,8},{7,5},{8,10},{9,7},{10,... | collective-permute-start | bytes 1572872 | tf_op jit(solution)/shard_map/ppermute | solution.py:375
  60.6 12.0 %collective-permute-start.12 = (bf16[4,256,256]{2,1,0:T(8,128)(2,1)S(1)}, bf16[4,256,256]{2,1,0:T(8,128)(2,1)S(1)}, u32[]{:S(2)}, u32[]{:S(2)}) collective-permute-start(bf16[4,256,256]{2,1,0:T(8,128)(2,1)S(1)} %collective-permute-done.7.refs_7_), channel_id=1, source_target_pairs={{0,32},{1,97},{2,34},{3,99},{4,36},{5,101},{6,38},{7,103},{8,40},{... | collective-permute-start | bytes 1572872 | tf_op jit(solution)/shard_map/ppermute | solution.py:375
  71.0 10.4 %collective-permute-start.11 = (bf16[4,256,256]{2,1,0:T(8,128)(2,1)S(1)}, bf16[4,256,256]{2,1,0:T(8,128)(2,1)S(1)}, u32[]{:S(2)}, u32[]{:S(2)}) collective-permute-start(bf16[4,256,256]{2,1,0:T(8,128)(2,1)S(1)} %collective-permute-done.9.refs_7_), channel_id=1, source_target_pairs={{0,2},{1,31},{2,4},{3,1},{4,6},{5,3},{6,8},{7,5},{8,10},{9,7},{10,... | collective-permute-start | bytes 1572872 | tf_op jit(solution)/shard_map/ppermute | solution.py:375
  71.0 12.0 %collective-permute-start.14 = (bf16[4,256,256]{2,1,0:T(8,128)(2,1)S(1)}, bf16[4,256,256]{2,1,0:T(8,128)(2,1)S(1)}, u32[]{:S(2)}, u32[]{:S(2)}) collective-permute-start(bf16[4,256,256]{2,1,0:T(8,128)(2,1)S(1)} %collective-permute-done.9.refs_7_), channel_id=1, source_target_pairs={{0,32},{1,97},{2,34},{3,99},{4,36},{5,101},{6,38},{7,103},{8,40},{... | collective-permute-start | bytes 1572872 | tf_op jit(solution)/shard_map/ppermute | solution.py:375
  81.4 10.4 %collective-permute-start.16 = (bf16[4,256,256]{2,1,0:T(8,128)(2,1)S(1)}, bf16[4,256,256]{2,1,0:T(8,128)(2,1)S(1)}, u32[]{:S(2)}, u32[]{:S(2)}) collective-permute-start(bf16[4,256,256]{2,1,0:T(8,128)(2,1)S(1)} %collective-permute-done.11.refs_7_), channel_id=1, source_target_pairs={{0,32},{1,97},{2,34},{3,99},{4,36},{5,101},{6,38},{7,103},{8,40},{... | collective-permute-start | bytes 1572872 | tf_op jit(solution)/shard_map/ppermute | solution.py:375
  83.0 10.4 %collective-permute-start.13 = (bf16[4,256,256]{2,1,0:T(8,128)(2,1)S(1)}, bf16[4,256,256]{2,1,0:T(8,128)(2,1)S(1)}, u32[]{:S(2)}, u32[]{:S(2)}) collective-permute-start(bf16[4,256,256]{2,1,0:T(8,128)(2,1)S(1)} %collective-permute-done.11.refs_7_), channel_id=1, source_target_pairs={{0,2},{1,31},{2,4},{3,1},{4,6},{5,3},{6,8},{7,5},{8,10},{9,7},{10,... | collective-permute-start | bytes 1572872 | tf_op jit(solution)/shard_map/ppermute | solution.py:375
  93.4 10.4 %collective-permute-start.15 = (bf16[4,256,256]{2,1,0:T(8,128)(2,1)S(1)}, bf16[4,256,256]{2,1,0:T(8,128)(2,1)S(1)}, u32[]{:S(2)}, u32[]{:S(2)}) collective-permute-start(bf16[4,256,256]{2,1,0:T(8,128)(2,1)S(1)} %collective-permute-done.13.refs_7_), channel_id=1, source_target_pairs={{0,2},{1,31},{2,4},{3,1},{4,6},{5,3},{6,8},{7,5},{8,10},{9,7},{10,... | collective-permute-start | bytes 1572872 | tf_op jit(solution)/shard_map/ppermute | solution.py:375
  98.2 31.2 %collective-permute-start.21 = (f32[48,64,128]{2,1,0:T(8,128)S(1)}, f32[48,64,128]{2,1,0:T(8,128)S(1)}, u32[]{:S(2)}, u32[]{:S(2)}) collective-permute-start(f32[48,64,128]{2,1,0:T(8,128)S(1)} %get-tuple-element.95), channel_id=1, source_target_pairs={{0,1},{1,0},{2,3},{3,2},{4,5},{5,4},{6,7},{7,6},{8,9},{9,8},{10,11... | collective-permute-start | bytes 4718600 | tf_op jit(solution)/shard_map/ppermute | solution.py:375
  98.3 10.5 %collective-permute-start.18 = (bf16[4,256,256]{2,1,0:T(8,128)(2,1)S(1)}, bf16[4,256,256]{2,1,0:T(8,128)(2,1)S(1)}, u32[]{:S(2)}, u32[]{:S(2)}) collective-permute-start(bf16[4,256,256]{2,1,0:T(8,128)(2,1)S(1)} %collective-permute-done.13.refs_7_), channel_id=1, source_target_pairs={{0,32},{1,97},{2,34},{3,99},{4,36},{5,101},{6,38},{7,103},{8,40},{... | collective-permute-start | bytes 1572872 | tf_op jit(solution)/shard_map/ppermute | solution.py:375
  103.8 10.7 %collective-permute-start.20 = (bf16[4,256,256]{2,1,0:T(8,128)(2,1)S(1)}, bf16[4,256,256]{2,1,0:T(8,128)(2,1)S(1)}, u32[]{:S(2)}, u32[]{:S(2)}) collective-permute-start(bf16[4,256,256]{2,1,0:T(8,128)(2,1)S(1)} %collective-permute-done.15.refs_7_), channel_id=1, source_target_pairs={{0,32},{1,97},{2,34},{3,99},{4,36},{5,101},{6,38},{7,103},{8,40},{... | collective-permute-start | bytes 1572872 | tf_op jit(solution)/shard_map/ppermute | solution.py:375
  105.4 10.4 %collective-permute-start.17 = (bf16[4,256,256]{2,1,0:T(8,128)(2,1)S(1)}, bf16[4,256,256]{2,1,0:T(8,128)(2,1)S(1)}, u32[]{:S(2)}, u32[]{:S(2)}) collective-permute-start(bf16[4,256,256]{2,1,0:T(8,128)(2,1)S(1)} %collective-permute-done.15.refs_7_), channel_id=1, source_target_pairs={{0,2},{1,31},{2,4},{3,1},{4,6},{5,3},{6,8},{7,5},{8,10},{9,7},{10,... | collective-permute-start | bytes 1572872 | tf_op jit(solution)/shard_map/ppermute | solution.py:375
  115.8 10.4 %collective-permute-start.19 = (bf16[4,256,256]{2,1,0:T(8,128)(2,1)S(1)}, bf16[4,256,256]{2,1,0:T(8,128)(2,1)S(1)}, u32[]{:S(2)}, u32[]{:S(2)}) collective-permute-start(bf16[4,256,256]{2,1,0:T(8,128)(2,1)S(1)} %collective-permute-done.17.refs_7_), channel_id=1, source_target_pairs={{0,32},{1,97},{2,34},{3,99},{4,36},{5,101},{6,38},{7,103},{8,40},{... | collective-permute-start | bytes 1572872 | tf_op jit(solution)/shard_map/ppermute | solution.py:375
  122.6 6.7 %collective-permute-start.22 = (f32[16,64,128]{2,1,0:T(8,128)S(1)}, f32[16,64,128]{2,1,0:T(8,128)S(1)}, u32[]{:S(2)}, u32[]{:S(2)}) collective-permute-start(f32[16,64,128]{2,1,0:T(8,128)S(1)} %get-tuple-element.96), channel_id=1, source_target_pairs={{0,1},{1,0},{2,3},{3,2},{4,5},{5,4},{6,7},{7,6},{8,9},{9,8},{10,11... | collective-permute-start | bytes 1572872 | tf_op jit(solution)/shard_map/ppermute | solution.py:375
